TPU v7x, 32 devices: a whole 2x2x4 slice. The times are simulated.
32 devices in a mesh: rows: 32 (over z, y, x, core).
Axes of the slice: x: 2, y: 2, z: 4, core: 2. Of those that a mesh axis runs over, the one named last changes fastest.
Arguments:
- wave_fn: float32 [512, 4, 4, 512], P('rows')
- left_env: bfloat16 [32, 512, 512], P(None, 'rows')
- op_pair: bfloat16 [32, 16, 16], replicated
- right_env: bfloat16 [32, 512, 512], replicated
Outputs:
- output 1: float32 [7, 512, 4, 4, 512], P(None, 'rows')
- output 2: float32 [6], replicated
- output 3: float32 [6], replicated
All inputs are finite; a program needn't handle non-finite values.
Results may differ from a plain program's by a relative error of at most 0.0119439.
Values are sent between devices in bfloat16 or wider.
A program may use at most 1 GiB of HBM per device.

v0:
```python
import jax
import jax.numpy as jnp
from jax import lax
from jax.sharding import PartitionSpec as P

NUM_STEPS = 6


def solution(mesh):
    row_axis = "rows"

    def local_run(wave_rows, left_rows, op_pair, right_env):
        local_rows = wave_rows.shape[0]
        phys_dim = wave_rows.shape[1]
        bond_dim = wave_rows.shape[3]
        num_terms = left_rows.shape[0]
        pair_dim = phys_dim * phys_dim
        vec_count = bond_dim * bond_dim * pair_dim
        right_flat = jnp.transpose(right_env, (0, 2, 1)).reshape(num_terms * bond_dim, bond_dim)

        def matvec(vec_rows):
            whole_vec = lax.all_gather(vec_rows.astype(jnp.bfloat16), row_axis, axis=0, tiled=True)
            flat_in = whole_vec.reshape(bond_dim, pair_dim * bond_dim)
            left_out = jnp.einsum("kap,pn->kan", left_rows, flat_in, preferred_element_type=jnp.float32)
            left_out = left_out.astype(jnp.bfloat16).reshape(num_terms, local_rows, pair_dim, bond_dim)
            mid_out = jnp.einsum("kqr,karc->aqkc", op_pair, left_out, preferred_element_type=jnp.float32)
            mid_out = mid_out.astype(jnp.bfloat16).reshape(local_rows * pair_dim, num_terms * bond_dim)
            sigma_rows = jnp.dot(mid_out, right_flat, preferred_element_type=jnp.float32)
            return sigma_rows.reshape(local_rows, phys_dim, phys_dim, bond_dim)

        def global_mean(local_val):
            return lax.psum(jnp.sum(local_val), row_axis) / vec_count

        first_vec = wave_rows / jnp.sqrt(global_mean(wave_rows * wave_rows))
        prev_vec = jnp.zeros_like(first_vec)
        cur_vec = first_vec
        beta_prev = jnp.zeros((), jnp.float32)
        vec_list = [first_vec]
        alpha_list = []
        beta_list = []
        for step_idx in range(NUM_STEPS):
            sigma_rows = matvec(cur_vec)
            alpha_val = global_mean(sigma_rows * cur_vec)
            resid_vec = sigma_rows - alpha_val * cur_vec - beta_prev * prev_vec
            beta_val = jnp.sqrt(global_mean(resid_vec * resid_vec))
            next_vec = resid_vec / beta_val
            vec_list.append(next_vec)
            alpha_list.append(alpha_val)
            beta_list.append(beta_val)
            prev_vec = cur_vec
            cur_vec = next_vec
            beta_prev = beta_val
        return jnp.stack(vec_list), jnp.stack(alpha_list), jnp.stack(beta_list)

    return jax.shard_map(local_run, mesh=mesh, in_specs=(P(row_axis), P(None, row_axis), P(), P()), out_specs=(P(None, row_axis), P(), P()), check_vma=False)
```

profile of v0, /device:TPU:0, one launch (start us, length us, event | category | flops | bytes accessed | tf_op | source)
XLA Modules:
  0.0 1528.2 jit_solution(17955346746907156154)
XLA Ops:
  9.2 42.1 %psum.91 = f32[]{:T(128)} all-reduce(f32[]{:T(128)} %multiply_reduce_fusion.12), channel_id=1, replica_groups=mesh['rows'=32] {'rows'}, use_global_device_ids=true, to_apply=%region_1.0 | all-reduce | flops 1 | bytes 8 | tf_op jit(solution)/shard_map/psum | solution.py:32
  55.1 22.6 %copy.34 = bf16[32,512,512]{1,2,0:T(8,128)(2,1)} copy(bf16[32,512,512]{2,1,0:T(8,128)(2,1)} %param.7) | data formatting | bytes 33554432 | tf_op args[3]
  77.7 54.2 %all-gather.7.cloned.1.call-done = bf16[512,4,4,512]{3,0,2,1:T(8,128)(2,1)} async-done(((bf16[16,4,4,512]{3,0,2,1:T(8,128)(2,1)}), bf16[512,4,4,512]{3,0,2,1:T(8,128)(2,1)}) %all-gather.7.cloned.1.call-update) | async-done | bytes 8388624 | tf_op jit(solution)/shard_map/all_gather | solution.py:22
  144.1 14.3 reshape.82
  224.9 40.2 %psum.92 = f32[]{:T(128)} all-reduce(f32[]{:T(128)} %get-tuple-element.21), channel_id=1, replica_groups=mesh['rows'=32] {'rows'}, use_global_device_ids=true, to_apply=%region_3.0 | all-reduce | flops 1 | bytes 8 | tf_op jit(solution)/shard_map/psum | solution.py:32
  266.7 39.4 %psum.93 = f32[]{:T(128)} all-reduce(f32[]{:T(128)} %multiply_reduce_fusion.10), channel_id=1, replica_groups=mesh['rows'=32] {'rows'}, use_global_device_ids=true, to_apply=%region_5.0 | all-reduce | flops 1 | bytes 8 | tf_op jit(solution)/shard_map/psum | solution.py:32
  307.9 78.0 %all-gather.9.cloned.1.call-done = bf16[512,4,4,512]{3,0,2,1:T(8,128)(2,1)} async-done(((bf16[16,4,4,512]{3,0,2,1:T(8,128)(2,1)}), bf16[512,4,4,512]{3,0,2,1:T(8,128)(2,1)}) %all-gather.9.cloned.1.call-update) | async-done | bytes 8388624 | tf_op jit(solution)/shard_map/all_gather | solution.py:22
  465.8 40.2 %psum.94 = f32[]{:T(128)} all-reduce(f32[]{:T(128)} %get-tuple-element.23), channel_id=1, replica_groups=mesh['rows'=32] {'rows'}, use_global_device_ids=true, to_apply=%region_7.0 | all-reduce | flops 1 | bytes 8 | tf_op jit(solution)/shard_map/psum | solution.py:32
  507.6 39.4 %psum.95 = f32[]{:T(128)} all-reduce(f32[]{:T(128)} %get-tuple-element.17), channel_id=1, replica_groups=mesh['rows'=32] {'rows'}, use_global_device_ids=true, to_apply=%region_9.0 | all-reduce | flops 1 | bytes 8 | tf_op jit(solution)/shard_map/psum | solution.py:32
  548.6 78.0 %all-gather.11.cloned.1.call-done = bf16[512,4,4,512]{3,0,2,1:T(8,128)(2,1)} async-done(((bf16[16,4,4,512]{3,0,2,1:T(8,128)(2,1)}), bf16[512,4,4,512]{3,0,2,1:T(8,128)(2,1)}) %all-gather.11.cloned.1.call-update) | async-done | bytes 8388624 | tf_op jit(solution)/shard_map/all_gather | solution.py:22
  681.2 13.9 dot_general.76
  706.2 40.2 %psum.96 = f32[]{:T(128)} all-reduce(f32[]{:T(128)} %get-tuple-element.25), channel_id=1, replica_groups=mesh['rows'=32] {'rows'}, use_global_device_ids=true, to_apply=%region_11.0 | all-reduce | flops 1 | bytes 8 | tf_op jit(solution)/shard_map/psum | solution.py:32
  747.9 39.4 %psum.97 = f32[]{:T(128)} all-reduce(f32[]{:T(128)} %get-tuple-element.15), channel_id=1, replica_groups=mesh['rows'=32] {'rows'}, use_global_device_ids=true, to_apply=%region_13.0 | all-reduce | flops 1 | bytes 8 | tf_op jit(solution)/shard_map/psum | solution.py:32
  788.9 78.0 %all-gather.13.cloned.1.call-done = bf16[512,4,4,512]{3,0,2,1:T(8,128)(2,1)} async-done(((bf16[16,4,4,512]{3,0,2,1:T(8,128)(2,1)}), bf16[512,4,4,512]{3,0,2,1:T(8,128)(2,1)}) %all-gather.13.cloned.1.call-update) | async-done | bytes 8388624 | tf_op jit(solution)/shard_map/all_gather | solution.py:22
  921.6 13.9 dot_general.80
  946.6 40.2 %psum.98 = f32[]{:T(128)} all-reduce(f32[]{:T(128)} %get-tuple-element.27), channel_id=1, replica_groups=mesh['rows'=32] {'rows'}, use_global_device_ids=true, to_apply=%region_15.0 | all-reduce | flops 1 | bytes 8 | tf_op jit(solution)/shard_map/psum | solution.py:32
  988.3 39.4 %psum.99 = f32[]{:T(128)} all-reduce(f32[]{:T(128)} %get-tuple-element.13), channel_id=1, replica_groups=mesh['rows'=32] {'rows'}, use_global_device_ids=true, to_apply=%region_17.0 | all-reduce | flops 1 | bytes 8 | tf_op jit(solution)/shard_map/psum | solution.py:32
  1029.3 78.0 %all-gather.15.cloned.1.call-done = bf16[512,4,4,512]{3,0,2,1:T(8,128)(2,1)} async-done(((bf16[16,4,4,512]{3,0,2,1:T(8,128)(2,1)}), bf16[512,4,4,512]{3,0,2,1:T(8,128)(2,1)}) %all-gather.15.cloned.1.call-update) | async-done | bytes 8388624 | tf_op jit(solution)/shard_map/all_gather | solution.py:22
  1175.5 14.1 multiply_reduce_fusion.3
  1189.7 40.2 %psum.100 = f32[]{:T(128)} all-reduce(f32[]{:T(128)} %get-tuple-element.29), channel_id=1, replica_groups=mesh['rows'=32] {'rows'}, use_global_device_ids=true, to_apply=%region_19.0 | all-reduce | flops 1 | bytes 8 | tf_op jit(solution)/shard_map/psum | solution.py:32
  1232.4 39.4 %psum.101 = f32[]{:T(128)} all-reduce(f32[]{:T(128)} %get-tuple-element.11), channel_id=1, replica_groups=mesh['rows'=32] {'rows'}, use_global_device_ids=true, to_apply=%region_21.0 | all-reduce | flops 1 | bytes 8 | tf_op jit(solution)/shard_map/psum | solution.py:32
  1279.8 71.6 %all-gather.17.cloned.1.call-done = bf16[512,4,4,512]{3,0,2,1:T(8,128)(2,1)} async-done(((bf16[16,4,4,512]{3,0,2,1:T(8,128)(2,1)}), bf16[512,4,4,512]{3,0,2,1:T(8,128)(2,1)}) %all-gather.17.cloned.1.call-update) | async-done | bytes 8388624 | tf_op jit(solution)/shard_map/all_gather | solution.py:22
  1431.0 40.2 %psum.102 = f32[]{:T(128)} all-reduce(f32[]{:T(128)} %get-tuple-element.31), channel_id=1, replica_groups=mesh['rows'=32] {'rows'}, use_global_device_ids=true, to_apply=%region_23.0 | all-reduce | flops 1 | bytes 8 | tf_op jit(solution)/shard_map/psum | solution.py:32
  1472.7 39.4 %psum.103 = f32[]{:T(128)} all-reduce(f32[]{:T(128)} %get-tuple-element.9), channel_id=1, replica_groups=mesh['rows'=32] {'rows'}, use_global_device_ids=true, to_apply=%region_25.0 | all-reduce | flops 1 | bytes 8 | tf_op jit(solution)/shard_map/psum | solution.py:32
  (83 shorter events, 468.3 us)
Async XLA Ops:
  7.2 151.3 %copy-start = (bf16[32,16,512]{2,1,0:T(8,128)(2,1)S(1)}, bf16[32,16,512]{2,1,0:T(8,128)(2,1)}, u32[]{:S(2)}) copy-start(bf16[32,16,512]{2,1,0:T(8,128)(2,1)} %param.5) | copy-start | bytes 1572868
  7.2 124.7 %all-gather.7.cloned.1.call-start = ((), (), s32[]{:S(2)}) async-start(), calls=%async_computation | async-start | bytes 8650752 | tf_op jit(solution)/shard_map/all_gather | solution.py:22
  54.1 331.9 %all-gather.9.cloned.1.call-start = ((), (), s32[]{:S(2)}) async-start(), calls=%async_computation.1 | async-start | bytes 8650752 | tf_op jit(solution)/shard_map/all_gather | solution.py:22
  199.9 13.7 copy-start.1
  307.9 439.2 %copy-start.3 = (f32[16,4,4,512]{3,0,2,1:T(8,128)}, f32[16,4,4,512]{3,0,2,1:T(8,128)S(1)}, u32[]{:S(2)}) copy-start(f32[16,4,4,512]{3,0,2,1:T(8,128)S(1)} %get-tuple-element.20) | copy-start | bytes 1572868
  307.9 318.7 %all-gather.11.cloned.1.call-start = ((), (), s32[]{:S(2)}) async-start(), calls=%async_computation.2 | async-start | bytes 8650752 | tf_op jit(solution)/shard_map/all_gather | solution.py:22
  548.5 318.3 %all-gather.13.cloned.1.call-start = ((), (), s32[]{:S(2)}) async-start(), calls=%async_computation.3 | async-start | bytes 8650752 | tf_op jit(solution)/shard_map/all_gather | solution.py:22
  788.8 318.5 %all-gather.15.cloned.1.call-start = ((), (), s32[]{:S(2)}) async-start(), calls=%async_computation.4 | async-start | bytes 8650752 | tf_op jit(solution)/shard_map/all_gather | solution.py:22
  1029.2 322.1 %all-gather.17.cloned.1.call-start = ((), (), s32[]{:S(2)}) async-start(), calls=%async_computation.5 | async-start | bytes 8650752 | tf_op jit(solution)/shard_map/all_gather | solution.py:22
  1175.5 97.7 %copy-start.2 = (f32[16,4,4,512]{3,2,1,0:T(4,128)S(1)}, f32[16,4,4,512]{3,2,1,0:T(4,128)}, u32[]{:S(2)}) copy-start(f32[16,4,4,512]{3,2,1,0:T(4,128)} %param.4) | copy-start | bytes 1572868
Sparse Core Ops, SparseCore 0:
  54.2 77.6 all-gather.6
  308.0 77.8 all-gather.8
  548.6 77.8 all-gather.10
  788.9 77.8 all-gather.12
  1029.3 77.8 all-gather.14
  1273.4 77.8 all-gather.16
where the time goes:
time: 1540 us; the launch traced here: 1530 us
  blocking collectives  520 us (34%)
  waiting for transfers between devices  438 us (28%)
  local copies, waits for them, and re-layouts  342 us (22%)
  matrix products  185 us (12%)
  between operations  23.3 us (2%)
  other arithmetic  19.6 us (1%)
    psum x13, blocking collectives, global_mean(): return lax.psum(jnp.sum(local_val), row_axis) / vec_count  520 us
    all_gather x6, waiting for transfers between devices, matvec(): lax.all_gather(vec_rows.astype(jnp.bfloat16), row_axis, axis=0, tiled=True)  438 us
    unnamed x18, local copies, waits for them, and re-layouts  97.6 us
    dot_general x6, local copies, waits for them, and re-layouts, matvec(): jnp.dot(mid_out, right_flat, preferred_element_type=jnp.float32)  82.3 us
    all_gather x6, local copies, waits for them, and re-layouts, matvec(): lax.all_gather(vec_rows.astype(jnp.bfloat16), row_axis, axis=0, tiled=True)  78.4 us
    dot_general x6, matrix products, matvec(): jnp.dot(mid_out, right_flat, preferred_element_type=jnp.float32)  70 us
    convert_element_type x6, local copies, waits for them, and re-layouts, matvec(): mid_out.astype(jnp.bfloat16)  68 us
    dot_general x6, matrix products, matvec(): jnp.einsum('kap,pn->kan', left_rows, flat_in, preferred_element_type=jnp....  61.8 us
  transfers between devices with their start and end apart: 6, of which 6 were waited for; matrix products, arithmetic and copies ran while one was open for 2% of the time, Pallas kernels for 0%

commit v1 on v0

v1 whole, which is shorter than its diff:
```python
import functools

import jax
import jax.numpy as jnp
from jax import lax
from jax.experimental import pallas as pl
from jax.experimental.pallas import tpu as pltpu
from jax.sharding import PartitionSpec as P

NUM_STEPS = 6
MESH = pl.DeviceIdType.MESH
F32 = jnp.float32
BF16 = jnp.bfloat16


def lanczos_kernel(
    vec_count,
    psi_ref, left_ref, op_ref, right_ref,
    out_ref, alpha_ref, beta_ref,
    u_ref, stage_ref, env_l, env_r, kron_ref, x_ref, y_ref, sig_ref, part_ref, v_ref, w_ref, stat_ref,
    recv_sem, send_sem, pair_send, pair_recv, part_sem, stat_sem, load_sem, out_sem,
):
    idx = lax.axis_index("rows")
    core = lax.rem(idx, 2)
    pos_x = lax.rem(idx // 2, 2)
    pos_y = lax.rem(idx // 4, 2)
    pos_z = idx // 8
    chip = idx // 2
    sib = idx + 1 - 2 * core
    next_x = idx + 2 - 4 * pos_x
    next_y = idx + 4 - 8 * pos_y

    def block(cc, half, src):
        return u_ref.at[cc, pl.ds(4 * half, 4), pl.ds(pl.multiple_of(32 * src, 32), 32), :]

    def copy(cc, half, src, target, way):
        return pltpu.make_async_remote_copy(
            src_ref=block(cc, half, src), dst_ref=block(cc, half, src),
            send_sem=send_sem.at[way], recv_sem=recv_sem.at[src, 2 * cc + half],
            device_id=(target,), device_id_type=MESH)

    def arrived(cc, half, src):
        copy(cc, half, src, sib, 0).wait_recv()

    def chip_at(px, py, pz):
        return (pz * 2 + py) * 2 + px

    def send_x(cc, half, src):
        copy(cc, half, src, next_x, 0).start()

    def send_y(cc, half, src):
        copy(cc, half, src, next_y, 1).start()

    def send_up(cc, src):
        @pl.when(pos_z < 3)
        def _():
            for half in range(2):
                copy(cc, half, src, idx + 8, 2).start()

    def send_down(cc, src):
        @pl.when(pos_z > 0)
        def _():
            for half in range(2):
                copy(cc, half, src, idx - 8, 3).start()

    def at_distance(dist, act):
        if dist == 0:
            act(pos_z, 0)
            return

        @pl.when(pos_z >= dist)
        def _():
            act(pos_z - dist, 1)

        @pl.when(pos_z + dist <= 3)
        def _():
            act(pos_z + dist, -1)

    def own_z(cc):
        send_up(cc, chip)
        send_down(cc, chip)

    def column_xy(cc, dist):
        def act(pz, _):
            src = chip_at(pos_x, pos_y, pz)
            for half in range(2):
                send_x(cc, half, src)
                send_y(cc, half, src)
        at_distance(dist, act)

    def from_z(cc, dist):
        def act(pz, way):
            src = chip_at(pos_x, pos_y, pz)
            for half in range(2):
                arrived(cc, half, src)
            if way > 0:
                send_up(cc, src)
            else:
                send_down(cc, src)
        at_distance(dist, act)

    def from_xy(cc, dist):
        def act(pz, _):
            src_x = chip_at(1 - pos_x, pos_y, pz)
            src_y = chip_at(pos_x, 1 - pos_y, pz)
            arrived(cc, 0, src_x)
            send_y(cc, 0, src_x)
            arrived(cc, 1, src_y)
            send_x(cc, 1, src_y)
            arrived(cc, 1, src_x)
            arrived(cc, 0, src_y)
        at_distance(dist, act)

    def from_diag(cc):
        for pz in range(4):
            src = chip_at(1 - pos_x, 1 - pos_y, pz)
            for half in range(2):
                arrived(cc, half, src)

    def sends_done():
        def blocks(count):
            return u_ref.at[:, :, pl.ds(0, 32 * count), :]

        def wait(count, way):
            pltpu.make_async_copy(blocks(count), blocks(count), send_sem.at[way]).wait()

        wait(6, 0)
        wait(6, 1)
        for pz in range(4):
            @pl.when(pos_z == pz)
            def _():
                if pz < 3:
                    wait(pz + 1, 2)
                if pz > 0:
                    wait(4 - pz, 3)

    my_rows = pl.ds(pl.multiple_of(32 * chip + 16 * core, 16), 16)
    right_loads = [
        pltpu.make_async_copy(
            right_ref.at[:, pl.ds(pl.multiple_of(256 * core + 128 * cc, 128), 128), :], env_r.at[cc], load_sem.at[cc])
        for cc in range(2)]
    left_load = pltpu.make_async_copy(left_ref, env_l.at[:, core], load_sem.at[2])
    left_send = pltpu.make_async_remote_copy(
        src_ref=left_ref, dst_ref=env_l.at[:, core], send_sem=load_sem.at[3], recv_sem=load_sem.at[4],
        device_id=(sib,), device_id_type=MESH)
    left_send.start()
    left_load.start()
    for load in right_loads:
        load.start()

    def build_kron():
        row_id = lax.broadcasted_iota(jnp.int32, (256, 16), 0)
        col_id = lax.broadcasted_iota(jnp.int32, (256, 16), 1)
        spread = jnp.where(lax.shift_right_logical(row_id, 4) == col_id, 1.0, 0.0).astype(BF16)
        big_row = lax.broadcasted_iota(jnp.int32, (256, 256), 0)
        big_col = lax.broadcasted_iota(jnp.int32, (256, 256), 1)
        same = (big_row & 15) == (big_col & 15)

        def one(k, carry):
            tall = jnp.dot(spread, op_ref[k], preferred_element_type=F32).astype(BF16)
            full = lax.dot_general(tall, spread, (((1,), (1,)), ((), ())), preferred_element_type=F32)
            kron_ref[k] = jnp.where(same, full, 0.0).astype(BF16)
            return carry

        lax.fori_loop(0, 32, one, 0)

    def x_stage(cc):
        def one(rp, carry):
            out = jnp.dot(env_l[...].reshape(1024, 512), u_ref[cc, rp], preferred_element_type=F32)
            out = out.astype(BF16).reshape(32, 2, 16, 256)
            for ag in range(2):
                for par in range(2):
                    rows = pl.ds(pl.multiple_of((2 * rp + par) * 16, 16), 16)
                    x_ref[:, rows, ag * 128:(ag + 1) * 128] = out[:, ag, :, par * 128:(par + 1) * 128]
            return carry

        lax.fori_loop(0, 8, one, 0)

    def y_stage():
        def one(k4, carry):
            for kk in range(4):
                k = k4 * 4 + kk
                out = jnp.dot(kron_ref[k], x_ref[k], preferred_element_type=F32).astype(BF16)
                lanes = pl.ds(pl.multiple_of(k4 * 512 + kk * 128, 128), 128)
                for ag in range(2):
                    y_ref[ag, :, lanes] = out[:, ag * 128:(ag + 1) * 128]
            return carry

        lax.fori_loop(0, 8, one, 0)

    def s_stage(cc, ag):
        return jnp.dot(y_ref[ag], env_r[cc].reshape(4096, 512), preferred_element_type=F32)

    def exchange_stats():
        def stat_copy(target):
            return pltpu.make_async_remote_copy(
                src_ref=stat_ref.at[idx], dst_ref=stat_ref.at[idx], send_sem=stat_sem.at[0], recv_sem=stat_sem.at[1],
                device_id=(target,), device_id_type=MESH)

        def send(off, carry):
            stat_copy(lax.rem(idx + off, 32)).start()
            return carry

        lax.fori_loop(1, 32, send, 0)
        others = stat_ref.at[pl.ds(0, 31)]
        pltpu.make_async_copy(others, others, stat_sem.at[1]).wait()
        pltpu.make_async_copy(others, others, stat_sem.at[0]).wait()
        lane = lax.broadcasted_iota(jnp.int32, (1, 128), 1)

        def pick(row, which):
            return jnp.sum(jnp.where(lane == which, row, 0.0))

        rows = [stat_ref[d] for d in range(32)]
        total = rows[0]
        for row in rows[1:]:
            total = total + row
        alpha = pick(total, 0) / vec_count
        extra = jnp.zeros((1, 128), F32)
        for row in rows:
            delta = alpha - pltpu.roll(row, 2, 1)
            extra = extra + delta * (delta * row - 2.0 * pltpu.roll(row, 127, 1))
        beta_vec = jnp.sqrt(jnp.full((1, 128), (pick(total, 2) + pick(extra, 3)) / vec_count, F32))
        return alpha, jnp.max(beta_vec)

    def put_stats(dot_val, proj, sq_w, sq_v, cross):
        lane = lax.broadcasted_iota(jnp.int32, (1, 128), 1)
        row = jnp.zeros((1, 128), F32)
        for which, val in enumerate((dot_val, proj, sq_w, sq_v, cross)):
            row = jnp.where(lane == which, val, row)
        stat_ref[idx] = row

    def fold(val):
        return jnp.sum(val.reshape(2, 8, 512), axis=0)

    def normalise(slot, prev, alpha, beta, proj):
        delta = alpha - proj
        beta_row = jnp.full((1, 512), beta, F32)

        def one(q, carry):
            rows = pl.ds(pl.multiple_of(q * 16, 16), 16)
            v_ref[slot, rows, :] = (w_ref[rows, :] - delta * v_ref[prev, rows, :]) / beta_row
            return carry

        lax.fori_loop(0, 16, one, 0)

    def out_copy(step, slot):
        return pltpu.make_async_copy(v_ref.at[slot], out_ref.at[step], out_sem)

    zero_acc = jnp.zeros((8, 512), F32)

    def first(q, acc):
        rows = pl.ds(pl.multiple_of(q * 16, 16), 16)
        val = psi_ref[rows, :]
        w_ref[rows, :] = val
        v_ref[1, rows, :] = jnp.zeros((16, 512), F32)
        v_ref[2, rows, :] = jnp.zeros((16, 512), F32)
        return acc + fold(val * val)

    acc = lax.fori_loop(0, 16, first, zero_acc)
    put_stats(0.0, 0.0, jnp.sum(acc), 0.0, 0.0)

    def step_body(j, proj):
        cur = lax.rem(j, 3)
        prev = lax.rem(j + 2, 3)
        alpha, beta = exchange_stats()

        @pl.when(j > 0)
        def _():
            alpha_ref[j - 1] = alpha
            beta_ref[j - 1] = beta
            out_copy(j - 1, prev).wait()

        normalise(cur, prev, alpha, beta, proj)
        out_copy(j, cur).start()

        def to_bf16(rp, carry):
            for par in range(2):
                rows = pl.ds(pl.multiple_of((2 * rp + par) * 16, 16), 16)
                for cc in range(2):
                    own = pl.ds(pl.multiple_of(256 * core + 128 * cc, 128), 128)
                    far = pl.ds(pl.multiple_of(256 * (1 - core) + 128 * cc, 128), 128)
                    u_ref[cc, rp, my_rows, par * 128:(par + 1) * 128] = v_ref[cur, rows, own].astype(BF16)
                    stage_ref[cc, rp, :, par * 128:(par + 1) * 128] = v_ref[cur, rows, far].astype(BF16)
            return carry

        lax.fori_loop(0, 8, to_bf16, 0)

        def pair_copy(cc):
            return pltpu.make_async_remote_copy(
                src_ref=stage_ref.at[cc], dst_ref=u_ref.at[cc, :, my_rows, :],
                send_sem=pair_send.at[cc], recv_sem=pair_recv.at[cc], device_id=(sib,), device_id_type=MESH)

        for cc in range(2):
            pair_copy(cc).start()
        pair_copy(0).wait_recv()
        own_z(0)
        column_xy(0, 0)
        pair_copy(1).wait_recv()
        own_z(1)

        @pl.when(j == 0)
        def _():
            build_kron()

        from_z(0, 1)
        column_xy(0, 1)
        from_xy(0, 0)
        column_xy(1, 0)
        from_z(1, 1)
        from_z(0, 2)
        column_xy(0, 2)
        from_xy(0, 1)
        column_xy(1, 1)
        from_z(1, 2)
        from_z(0, 3)
        column_xy(0, 3)
        from_xy(0, 2)
        from_xy(1, 0)
        from_xy(0, 3)
        column_xy(1, 2)
        from_xy(1, 1)
        from_z(1, 3)
        column_xy(1, 3)
        from_xy(1, 2)
        from_diag(0)

        @pl.when(j == 0)
        def _():
            left_load.wait()
            left_send.wait()
            for load in right_loads:
                load.wait()

        x_stage(0)
        from_xy(1, 3)
        y_stage()
        sig_ref[0] = s_stage(0, 1 - core)
        sig_ref[1] = s_stage(0, core)
        from_diag(1)
        x_stage(1)
        y_stage()
        sig_ref[0] = sig_ref[0] + s_stage(1, 1 - core)
        part_copy = pltpu.make_async_remote_copy(
            src_ref=sig_ref.at[0], dst_ref=part_ref, send_sem=part_sem.at[0], recv_sem=part_sem.at[1],
            device_id=(sib,), device_id_type=MESH)
        part_copy.start()
        sig_ref[1] = sig_ref[1] + s_stage(1, core)
        part_copy.wait()
        for cc in range(2):
            pair_copy(cc).wait_send()
        sends_done()

        def dots(q, accs):
            rows = pl.ds(pl.multiple_of(q * 16, 16), 16)
            sig = sig_ref[1, rows, :] + part_ref[rows, :]
            vec = v_ref[cur, rows, :]
            w_ref[rows, :] = sig
            return accs[0] + fold(sig * vec), accs[1] + fold(vec * vec)

        acc_p, acc_v = lax.fori_loop(0, 16, dots, (zero_acc, zero_acc))
        dot_val = jnp.sum(acc_p)
        sq_v = jnp.sum(acc_v)
        proj_vec = jnp.full((1, 128), dot_val, F32) / jnp.full((1, 128), jnp.where(sq_v > 0.0, sq_v, 1.0), F32)
        new_proj = jnp.where(sq_v > 0.0, jnp.max(proj_vec), 0.0)
        beta_use = jnp.where(j > 0, beta, 0.0)

        def resid(q, accs):
            rows = pl.ds(pl.multiple_of(q * 16, 16), 16)
            vec = v_ref[cur, rows, :]
            res = w_ref[rows, :] - beta_use * v_ref[prev, rows, :] - new_proj * vec
            w_ref[rows, :] = res
            return accs[0] + fold(res * res), accs[1] + fold(res * vec)

        acc_w, acc_c = lax.fori_loop(0, 16, resid, (zero_acc, zero_acc))
        put_stats(dot_val, new_proj, jnp.sum(acc_w), sq_v, jnp.sum(acc_c))
        return new_proj

    proj = lax.fori_loop(0, NUM_STEPS, step_body, jnp.float32(0.0))
    alpha, beta = exchange_stats()
    alpha_ref[NUM_STEPS - 1] = alpha
    beta_ref[NUM_STEPS - 1] = beta
    out_copy(NUM_STEPS - 1, (NUM_STEPS - 1) % 3).wait()
    normalise(NUM_STEPS % 3, (NUM_STEPS - 1) % 3, alpha, beta, proj)
    last = out_copy(NUM_STEPS, NUM_STEPS % 3)
    last.start()
    last.wait()


def solution(mesh):
    def local_run(wave_rows, left_rows, op_pair, right_env):
        rows, phys, _, bond = wave_rows.shape
        pair = phys * phys
        vec_count = float(bond * bond * pair)
        psi = jnp.transpose(wave_rows.reshape(rows, pair, bond), (1, 0, 2)).reshape(pair * rows, bond)
        vecs, alpha, beta = pl.pallas_call(
            functools.partial(lanczos_kernel, vec_count),
            out_shape=(
                jax.ShapeDtypeStruct((NUM_STEPS + 1, pair * rows, bond), F32),
                jax.ShapeDtypeStruct((NUM_STEPS,), F32),
                jax.ShapeDtypeStruct((NUM_STEPS,), F32),
            ),
            in_specs=[
                pl.BlockSpec(memory_space=pltpu.VMEM),
                pl.BlockSpec(memory_space=pl.ANY),
                pl.BlockSpec(memory_space=pltpu.VMEM),
                pl.BlockSpec(memory_space=pl.ANY),
            ],
            out_specs=(
                pl.BlockSpec(memory_space=pl.ANY),
                pl.BlockSpec(memory_space=pltpu.SMEM),
                pl.BlockSpec(memory_space=pltpu.SMEM),
            ),
            scratch_shapes=[
                pltpu.VMEM((2, 8, 512, 256), BF16),
                pltpu.VMEM((2, 8, 16, 256), BF16),
                pltpu.VMEM((32, 2, 16, 512), BF16),
                pltpu.VMEM((2, 32, 128, 512), BF16),
                pltpu.VMEM((32, 256, 256), BF16),
                pltpu.VMEM((32, 256, 256), BF16),
                pltpu.VMEM((2, 256, 4096), BF16),
                pltpu.VMEM((2, 256, 512), F32),
                pltpu.VMEM((256, 512), F32),
                pltpu.VMEM((3, 256, 512), F32),
                pltpu.VMEM((256, 512), F32),
                pltpu.VMEM((32, 1, 128), F32),
                pltpu.SemaphoreType.DMA((16, 4)),
                pltpu.SemaphoreType.DMA((4,)),
                pltpu.SemaphoreType.DMA((2,)),
                pltpu.SemaphoreType.DMA((2,)),
                pltpu.SemaphoreType.DMA((2,)),
                pltpu.SemaphoreType.DMA((2,)),
                pltpu.SemaphoreType.DMA((5,)),
                pltpu.SemaphoreType.DMA,
            ],
            compiler_params=pltpu.CompilerParams(has_side_effects=True, vmem_limit_bytes=60 * 1024 * 1024),
        )(psi, left_rows, op_pair, right_env)
        vecs = vecs.reshape(NUM_STEPS + 1, pair, rows, bond).transpose(0, 2, 1, 3)
        return vecs.reshape(NUM_STEPS + 1, rows, phys, phys, bond), alpha, beta

    return jax.shard_map(
        local_run, mesh=mesh,
        in_specs=(P("rows"), P(None, "rows"), P(), P()),
        out_specs=(P(None, "rows"), P(), P()), check_vma=False)
```

time: 1540 us -> 391 us (0.25)
  blocking collectives: 520 us -> 0 us
  waiting for transfers between devices: 438 us -> 0 us
  Pallas kernels: 0 us -> 379 us
  local copies, waits for them, and re-layouts: 342 us -> 11.1 us
  matrix products: 185 us -> 0 us
  between operations: 23.3 us -> 0.66 us
  other arithmetic: 19.6 us -> 0 us
    psum x13 -> x0, blocking collectives: 520 us -> none  [global_mean(): return lax.psum(jnp.sum(local_val), row_axis) / vec_count]
    all_gather x6 -> x0, waiting for transfers between devices: 438 us -> none  [matvec(): lax.all_gather(vec_rows.astype(jnp.bfloat16), row_axis, axis=0, tiled=True)]
    pallas_call x0 -> x1, Pallas kernels: none -> 379 us  [local_run(): pl.pallas_call(functools.partial(lanczos_kernel, vec_count), out_shape=(j...]
    dot_general x18 -> x0, matrix products: 185 us -> none  [the longest x6 70 us: matvec(): jnp.dot(mid_out, right_flat, preferred_element_type=jnp.float32)]
    unnamed x18 -> x7, local copies, waits for them, and re-layouts: 97.6 us -> 2.68 us
    dot_general x6 -> x0, local copies, waits for them, and re-layouts: 82.3 us -> none  [matvec(): jnp.dot(mid_out, right_flat, preferred_element_type=jnp.float32)]
    all_gather x6 -> x0, local copies, waits for them, and re-layouts: 78.4 us -> none  [matvec(): lax.all_gather(vec_rows.astype(jnp.bfloat16), row_axis, axis=0, tiled=True)]
    convert_element_type x6 -> x0, local copies, waits for them, and re-layouts: 68 us -> none  [matvec(): mid_out.astype(jnp.bfloat16)]
  transfers between devices with their start and end apart: 6 -> 0, of which waited for: 6 -> 0; matrix products, arithmetic and copies ran while one was open for 2% -> 0% of each run, Pallas kernels for 0% -> 0%
where the time goes in v1:
time: 391 us
  Pallas kernels  379 us (97%)
  local copies, waits for them, and re-layouts  11.1 us (3%)
    pallas_call x1, Pallas kernels, local_run(): pl.pallas_call(functools.partial(lanczos_kernel, vec_count), out_shape=(j...  379 us

profile of v1, /device:TPU:0, one launch (start us, length us, event | category | flops | bytes accessed | tf_op | source)
XLA Modules:
  0.0 390.5 jit_solution(9113134643473485458)
XLA Ops:
  0.6 1.6 copy.8.op_ref
  2.3 2.1 copy.10
  4.4 378.8 %shard_map.67 = (f32[7,256,512]{2,1,0:T(8,128)}, f32[6]{0:T(128)}, f32[6]{0:T(128)}) custom-call(f32[256,512]{1,0:T(8,128)} %bitcast.11, bf16[32,16,512]{2,1,0:T(8,128)(2,1)} %left_ref.1, bf16[32,16,16]{2,1,0:T(8,128)(2,1)} %copy.8.op_ref, bf16[32,512,512]{2,1,0:T(8,128)(2,1)} %right_ref.1), custom_call_target="tpu_custom_call" | custom-call | tf_op jit(solution)/shard_map/pallas_call | solution.py:395
  383.2 0.0 copy-start.1
  383.2 0.0 copy-start
  383.3 6.3 %copy.11 = f32[7,16,4,4,512]{4,3,2,1,0:T(4,128)} copy(f32[7,16,4,4,512]{4,1,3,2,0:T(8,128)} %bitcast.10) | data formatting | bytes 7340032 | tf_op jit(solution)/shard_map/reshape | solution.py:438
  389.5 0.0 copy-done.1
  389.5 0.5 copy.14
  390.0 0.0 copy-done
  390.0 0.5 copy.15
Async XLA Ops:
  383.2 6.3 %copy-start.1 = (f32[6]{0:T(128)S(1)}, f32[6]{0:T(128)}, u32[]{:S(2)}) copy-start(f32[6]{0:T(128)} %get-tuple-element.13) | copy-start | bytes 76
  383.2 6.8 %copy-start = (f32[6]{0:T(128)S(1)}, f32[6]{0:T(128)}, u32[]{:S(2)}) copy-start(f32[6]{0:T(128)} %get-tuple-element.14) | copy-start | bytes 76

commit v2 on v1

--- a/solution.py
+++ b/solution.py
@@ -11,6 +11,78 @@
 MESH = pl.DeviceIdType.MESH
 F32 = jnp.float32
 BF16 = jnp.bfloat16
+
+ROUTES = ("xzy", "yzx", "zyx", "zxy", "zxy", "zyx", "yxz", "zxy")
+ORDER = (
+    ("own", 2, "y", 0), ("own", 4, "x", 0), ("own", 2, "z", 0), ("own", 0, "x", 0), ("own", 0, "z", 0),
+    ("own", 0, "y", 0), ("own", 1, "y", 0), ("own", 3, "y", 0), ("own", 3, "z", 0), ("own", 3, "x", 0),
+    ("own", 2, "x", 0), ("own", 1, "z", 0), ("ev", 2, 0, 1), ("ev", 0, 1, 0), ("ev", 4, 1, 0), ("ev", 0, 0, 1),
+    ("ev", 3, 0, 1), ("ev", 1, 2, 0), ("ev", 1, 0, 1), ("ev", 0, 1, 1), ("own", 4, "y", 0), ("own", 5, "x", 0),
+    ("own", 1, "x", 0), ("ev", 2, 2, 0), ("ev", 0, 0, 2), ("ev", 3, 0, 2), ("ev", 2, 2, 1), ("ev", 1, 0, 2),
+    ("ev", 2, 0, 2), ("own", 4, "z", 0), ("own", 6, "y", 0), ("ev", 0, 1, 2), ("ev", 1, 2, 1), ("ev", 3, 1, 2),
+    ("own", 5, "z", 0), ("ev", 3, 1, 1), ("ev", 1, 0, 3), ("own", 7, "z", 0), ("ev", 0, 0, 3), ("ev", 3, 0, 3),
+    ("own", 6, "x", 0), ("ev", 2, 0, 3), ("ev", 2, 3, 1), ("ev", 0, 2, 0), ("ev", 0, 3, 1), ("ev", 0, 3, 0),
+    ("own", 6, "z", 0), ("ev", 1, 2, 2), ("own", 7, "x", 0), ("ev", 0, 1, 3), ("ev", 0, 2, 2), ("ev", 1, 1, 3),
+    ("ev", 3, 1, 0), ("ev", 4, 0, 1), ("ev", 0, 3, 2), ("ev", 6, 0, 1), ("ev", 1, 1, 1), ("own", 5, "y", 0),
+    ("ev", 0, 2, 1), ("ev", 0, 2, 3), ("ev", 2, 2, 2), ("own", 7, "y", 0), ("ev", 1, 3, 0), ("ev", 2, 1, 2),
+    ("ev", 1, 3, 1), ("ev", 1, 2, 3), ("ev", 3, 2, 3), ("ev", 2, 1, 0), ("ev", 1, 1, 0), ("ev", 6, 2, 0),
+    ("ev", 3, 2, 2), ("ev", 5, 0, 1), ("ev", 2, 2, 3), ("ev", 0, 3, 3), ("ev", 3, 1, 3), ("ev", 4, 0, 2),
+    ("ev", 1, 3, 2), ("ev", 3, 2, 1), ("ev", 7, 0, 1), ("ev", 1, 3, 3), ("ev", 4, 0, 3), ("ev", 2, 1, 1),
+    ("ev", 4, 3, 0), ("ev", 3, 3, 1), ("ev", 6, 0, 2), ("ev", 6, 1, 0), ("ev", 1, 1, 2), ("left", 1, 0, 0),
+    ("ev", 7, 1, 0), ("ev", 2, 3, 0), ("ev", 3, 3, 2), ("ev", 3, 3, 3), ("ev", 2, 1, 3), ("ev", 7, 0, 2),
+    ("ev", 2, 3, 2), ("ev", 2, 3, 3), ("ev", 3, 3, 0), ("left", 0, 0, 0), ("ev", 5, 0, 2), ("ev", 5, 2, 0),
+    ("ev", 3, 2, 0), ("ev", 6, 2, 1), ("left", 3, 0, 0), ("ev", 7, 0, 3), ("left", 2, 0, 0), ("ev", 5, 0, 3),
+    ("ev", 6, 3, 0), ("ev", 6, 1, 1), ("mid", 0, 0, 0), ("ev", 6, 0, 3), ("ev", 7, 1, 1), ("ev", 5, 2, 1),
+    ("ev", 6, 2, 2), ("ev", 4, 1, 3), ("mid", 1, 0, 0), ("ev", 4, 1, 2), ("mid", 2, 0, 0), ("ev", 7, 2, 1),
+    ("mid", 3, 0, 0), ("ev", 5, 1, 0), ("ev", 4, 1, 1), ("ev", 6, 3, 1), ("ev", 5, 2, 2), ("ev", 7, 1, 3),
+    ("ev", 5, 1, 2), ("ev", 5, 2, 3), ("ev", 7, 1, 2), ("ev", 7, 2, 3), ("ev", 5, 1, 1), ("ev", 6, 1, 2),
+    ("ev", 4, 2, 3), ("right", 0, 0, 0), ("ev", 7, 3, 0), ("ev", 5, 3, 0), ("ev", 6, 3, 2), ("right", 1, 0, 0),
+    ("ev", 5, 3, 1), ("ev", 5, 3, 2), ("ev", 4, 3, 2), ("ev", 4, 2, 0), ("ev", 4, 2, 1), ("ev", 7, 2, 2),
+    ("ev", 7, 2, 0), ("ev", 6, 1, 3), ("ev", 4, 2, 2), ("ev", 5, 3, 3), ("ev", 5, 1, 3), ("left", 5, 0, 0),
+    ("ev", 7, 3, 1), ("ev", 4, 3, 3), ("ev", 7, 3, 3), ("ev", 4, 3, 1), ("left", 4, 0, 0), ("ev", 7, 3, 2),
+    ("left", 7, 0, 0), ("ev", 6, 2, 3), ("ev", 6, 3, 3), ("left", 6, 0, 0), ("mid", 4, 0, 0), ("mid", 5, 0, 0),
+    ("mid", 6, 0, 0), ("mid", 7, 0, 0), ("right", 2, 0, 0), ("right", 3, 0, 0),
+)
+
+
+def onward(route, cls, dist):
+    if route[0] == "z":
+        first, second = route[1], route[2]
+    elif route[2] == "z":
+        first, second = route[0], route[1]
+    else:
+        first, second = route[0], route[2]
+    bit = {"x": 1, "y": 2}
+    off_first, off_second = bool(cls & bit[first]), bool(cls & bit[second])
+    if route[0] == "z":
+        if cls == 0:
+            return ["z", first, second]
+        return [second] if off_first and not off_second else []
+    if route[2] == "z":
+        ways = []
+        if dist == 0 and cls == 0:
+            ways = [first, second]
+        elif dist == 0 and off_first and not off_second:
+            ways = [second]
+        return ways + ["z"]
+    if off_second:
+        return []
+    return ([first] if dist == 0 and not off_first else []) + [second, "z"]
+
+
+def sends_on(way, cc, pz):
+    count = 0
+    for piece in range(4 * cc, 4 * cc + 4):
+        for cls in range(4):
+            for src_z in range(4):
+                ways = onward(ROUTES[piece], cls, abs(pz - src_z))
+                if way in ("x", "y"):
+                    count += way in ways
+                elif way == "up":
+                    count += "z" in ways and src_z <= pz < 3
+                else:
+                    count += "z" in ways and src_z >= pz > 0
+    return count
 
 
 def lanczos_kernel(
@@ -30,109 +102,77 @@
     next_x = idx + 2 - 4 * pos_x
     next_y = idx + 4 - 8 * pos_y
 
-    def block(cc, half, src):
-        return u_ref.at[cc, pl.ds(4 * half, 4), pl.ds(pl.multiple_of(32 * src, 32), 32), :]
-
-    def copy(cc, half, src, target, way):
+    def block(piece, first_row, rows):
+        return u_ref.at[piece // 4, pl.ds(2 * (piece % 4), 2), pl.ds(pl.multiple_of(first_row, 16), rows), :]
+
+    WAYS = {"x": 0, "y": 1, "up": 2, "down": 3}
+
+    def copy(piece, src, way, first_row, rows):
+        target = {"x": next_x, "y": next_y, "up": idx + 8, "down": idx - 8}[way]
+        ref = block(piece, first_row, rows)
         return pltpu.make_async_remote_copy(
-            src_ref=block(cc, half, src), dst_ref=block(cc, half, src),
-            send_sem=send_sem.at[way], recv_sem=recv_sem.at[src, 2 * cc + half],
-            device_id=(target,), device_id_type=MESH)
-
-    def arrived(cc, half, src):
-        copy(cc, half, src, sib, 0).wait_recv()
-
-    def chip_at(px, py, pz):
-        return (pz * 2 + py) * 2 + px
-
-    def send_x(cc, half, src):
-        copy(cc, half, src, next_x, 0).start()
-
-    def send_y(cc, half, src):
-        copy(cc, half, src, next_y, 1).start()
-
-    def send_up(cc, src):
-        @pl.when(pos_z < 3)
-        def _():
-            for half in range(2):
-                copy(cc, half, src, idx + 8, 2).start()
-
-    def send_down(cc, src):
-        @pl.when(pos_z > 0)
-        def _():
-            for half in range(2):
-                copy(cc, half, src, idx - 8, 3).start()
-
-    def at_distance(dist, act):
+            src_ref=ref, dst_ref=ref, send_sem=send_sem.at[WAYS[way] + 4 * (piece // 4)],
+            recv_sem=recv_sem.at[src, piece], device_id=(target,), device_id_type=MESH)
+
+    def send(piece, src, way, first_row=None, rows=32):
+        if first_row is None:
+            first_row = 32 * src
+        if way == "up":
+            @pl.when(pos_z < 3)
+            def _():
+                copy(piece, src, way, first_row, rows).start()
+        elif way == "down":
+            @pl.when(pos_z > 0)
+            def _():
+                copy(piece, src, way, first_row, rows).start()
+        else:
+            copy(piece, src, way, first_row, rows).start()
+
+    def send_own(piece, way, first_row=None, rows=32):
+        for one in (("up", "down") if way == "z" else (way,)):
+            send(piece, chip, one, first_row, rows)
+
+    def arrival(piece, cls, dist):
+        col_x = 1 - pos_x if cls & 1 else pos_x
+        col_y = 1 - pos_y if cls & 2 else pos_y
+
+        def act(src_z, heading):
+            src = (src_z * 2 + col_y) * 2 + col_x
+            copy(piece, src, "x", 32 * src, 32).wait_recv()
+            for way in onward(ROUTES[piece], cls, dist):
+                if way != "z":
+                    send(piece, src, way)
+                else:
+                    for one in heading:
+                        send(piece, src, one)
+
         if dist == 0:
-            act(pos_z, 0)
+            act(pos_z, ("up", "down"))
             return
 
         @pl.when(pos_z >= dist)
         def _():
-            act(pos_z - dist, 1)
+            act(pos_z - dist, ("up",))
 
         @pl.when(pos_z + dist <= 3)
         def _():
-            act(pos_z + dist, -1)
-
-    def own_z(cc):
-        send_up(cc, chip)
-        send_down(cc, chip)
-
-    def column_xy(cc, dist):
-        def act(pz, _):
-            src = chip_at(pos_x, pos_y, pz)
-            for half in range(2):
-                send_x(cc, half, src)
-                send_y(cc, half, src)
-        at_distance(dist, act)
-
-    def from_z(cc, dist):
-        def act(pz, way):
-            src = chip_at(pos_x, pos_y, pz)
-            for half in range(2):
-                arrived(cc, half, src)
-            if way > 0:
-                send_up(cc, src)
-            else:
-                send_down(cc, src)
-        at_distance(dist, act)
-
-    def from_xy(cc, dist):
-        def act(pz, _):
-            src_x = chip_at(1 - pos_x, pos_y, pz)
-            src_y = chip_at(pos_x, 1 - pos_y, pz)
-            arrived(cc, 0, src_x)
-            send_y(cc, 0, src_x)
-            arrived(cc, 1, src_y)
-            send_x(cc, 1, src_y)
-            arrived(cc, 1, src_x)
-            arrived(cc, 0, src_y)
-        at_distance(dist, act)
-
-    def from_diag(cc):
-        for pz in range(4):
-            src = chip_at(1 - pos_x, 1 - pos_y, pz)
-            for half in range(2):
-                arrived(cc, half, src)
+            act(pos_z + dist, ("down",))
 
     def sends_done():
-        def blocks(count):
-            return u_ref.at[:, :, pl.ds(0, 32 * count), :]
-
-        def wait(count, way):
-            pltpu.make_async_copy(blocks(count), blocks(count), send_sem.at[way]).wait()
-
-        wait(6, 0)
-        wait(6, 1)
+        def wait(count, way, cc):
+            if count:
+                ref = env_r.at[0, pl.ds(0, count), pl.ds(0, 32), :]
+                pltpu.make_async_copy(ref, ref, send_sem.at[WAYS[way] + 4 * cc]).wait()
+
+        for cc in range(2):
+            wait(sends_on("x", cc, 0), "x", cc)
+            wait(sends_on("y", cc, 0), "y", cc)
         for pz in range(4):
             @pl.when(pos_z == pz)
             def _():
-                if pz < 3:
-                    wait(pz + 1, 2)
-                if pz > 0:
-                    wait(4 - pz, 3)
+                for cc in range(2):
+                    wait(sends_on("up", cc, pz), "up", cc)
+                    wait(sends_on("down", cc, pz), "down", cc)
 
     my_rows = pl.ds(pl.multiple_of(32 * chip + 16 * core, 16), 16)
     right_loads = [
@@ -164,32 +204,28 @@
 
         lax.fori_loop(0, 32, one, 0)
 
-    def x_stage(cc):
-        def one(rp, carry):
-            out = jnp.dot(env_l[...].reshape(1024, 512), u_ref[cc, rp], preferred_element_type=F32)
+    def left_part(piece):
+        for sub in range(2):
+            rp = 2 * (piece % 4) + sub
+            out = jnp.dot(env_l[...].reshape(1024, 512), u_ref[piece // 4, rp], preferred_element_type=F32)
             out = out.astype(BF16).reshape(32, 2, 16, 256)
             for ag in range(2):
                 for par in range(2):
-                    rows = pl.ds(pl.multiple_of((2 * rp + par) * 16, 16), 16)
-                    x_ref[:, rows, ag * 128:(ag + 1) * 128] = out[:, ag, :, par * 128:(par + 1) * 128]
-            return carry
-
-        lax.fori_loop(0, 8, one, 0)
-
-    def y_stage():
-        def one(k4, carry):
-            for kk in range(4):
-                k = k4 * 4 + kk
-                out = jnp.dot(kron_ref[k], x_ref[k], preferred_element_type=F32).astype(BF16)
-                lanes = pl.ds(pl.multiple_of(k4 * 512 + kk * 128, 128), 128)
-                for ag in range(2):
-                    y_ref[ag, :, lanes] = out[:, ag * 128:(ag + 1) * 128]
-            return carry
-
-        lax.fori_loop(0, 8, one, 0)
-
-    def s_stage(cc, ag):
-        return jnp.dot(y_ref[ag], env_r[cc].reshape(4096, 512), preferred_element_type=F32)
+                    row = (2 * rp + par) * 16
+                    x_ref[:, row:row + 16, ag * 128:(ag + 1) * 128] = out[:, ag, :, par * 128:(par + 1) * 128]
+
+    def mid_part(part):
+        for kk in range(8):
+            k = 8 * (part % 4) + kk
+            out = jnp.dot(kron_ref[k], x_ref[k], preferred_element_type=F32).astype(BF16)
+            for ag in range(2):
+                y_ref[ag, :, k * 128:(k + 1) * 128] = out[:, ag * 128:(ag + 1) * 128]
+
+    def right_part(part):
+        cc, who = part // 2, part % 2
+        ag = 1 - core if who == 0 else core
+        out = jnp.dot(y_ref[ag], env_r[cc].reshape(4096, 512), preferred_element_type=F32)
+        sig_ref[who] = out if cc == 0 else sig_ref[who] + out
 
     def exchange_stats():
         def stat_copy(target):
@@ -197,11 +233,11 @@
                 src_ref=stat_ref.at[idx], dst_ref=stat_ref.at[idx], send_sem=stat_sem.at[0], recv_sem=stat_sem.at[1],
                 device_id=(target,), device_id_type=MESH)
 
-        def send(off, carry):
+        def to_all(off, carry):
             stat_copy(lax.rem(idx + off, 32)).start()
             return carry
 
-        lax.fori_loop(1, 32, send, 0)
+        lax.fori_loop(1, 32, to_all, 0)
         others = stat_ref.at[pl.ds(0, 31)]
         pltpu.make_async_copy(others, others, stat_sem.at[1]).wait()
         pltpu.make_async_copy(others, others, stat_sem.at[0]).wait()
@@ -238,10 +274,11 @@
 
         def one(q, carry):
             rows = pl.ds(pl.multiple_of(q * 16, 16), 16)
-            v_ref[slot, rows, :] = (w_ref[rows, :] - delta * v_ref[prev, rows, :]) / beta_row
-            return carry
-
-        lax.fori_loop(0, 16, one, 0)
+            vec = (w_ref[rows, :] - delta * v_ref[prev, rows, :]) / beta_row
+            v_ref[slot, rows, :] = vec
+            return carry + fold(vec * vec)
+
+        return lax.fori_loop(0, 16, one, jnp.zeros((8, 512), F32))
 
     def out_copy(step, slot):
         return pltpu.make_async_copy(v_ref.at[slot], out_ref.at[step], out_sem)
@@ -270,7 +307,7 @@
             beta_ref[j - 1] = beta
             out_copy(j - 1, prev).wait()
 
-        normalise(cur, prev, alpha, beta, proj)
+        acc_v = normalise(cur, prev, alpha, beta, proj)
         out_copy(j, cur).start()
 
         def to_bf16(rp, carry):
@@ -292,59 +329,42 @@
 
         for cc in range(2):
             pair_copy(cc).start()
-        pair_copy(0).wait_recv()
-        own_z(0)
-        column_xy(0, 0)
-        pair_copy(1).wait_recv()
-        own_z(1)
+        lead = 0
+        while ORDER[lead][0] == "own":
+            lead += 1
+        for _, piece, way, _ in ORDER[:lead]:
+            send_own(piece, way, 32 * chip + 16 * core, 16)
+        for cc in range(2):
+            pair_copy(cc).wait_recv()
+            for _, piece, way, _ in ORDER[:lead]:
+                if piece // 4 == cc:
+                    send_own(piece, way, 32 * chip + 16 * (1 - core), 16)
+        sq_v = jnp.sum(acc_v)
 
         @pl.when(j == 0)
         def _():
             build_kron()
-
-        from_z(0, 1)
-        column_xy(0, 1)
-        from_xy(0, 0)
-        column_xy(1, 0)
-        from_z(1, 1)
-        from_z(0, 2)
-        column_xy(0, 2)
-        from_xy(0, 1)
-        column_xy(1, 1)
-        from_z(1, 2)
-        from_z(0, 3)
-        column_xy(0, 3)
-        from_xy(0, 2)
-        from_xy(1, 0)
-        from_xy(0, 3)
-        column_xy(1, 2)
-        from_xy(1, 1)
-        from_z(1, 3)
-        column_xy(1, 3)
-        from_xy(1, 2)
-        from_diag(0)
-
-        @pl.when(j == 0)
-        def _():
             left_load.wait()
             left_send.wait()
             for load in right_loads:
                 load.wait()
 
-        x_stage(0)
-        from_xy(1, 3)
-        y_stage()
-        sig_ref[0] = s_stage(0, 1 - core)
-        sig_ref[1] = s_stage(0, core)
-        from_diag(1)
-        x_stage(1)
-        y_stage()
-        sig_ref[0] = sig_ref[0] + s_stage(1, 1 - core)
         part_copy = pltpu.make_async_remote_copy(
             src_ref=sig_ref.at[0], dst_ref=part_ref, send_sem=part_sem.at[0], recv_sem=part_sem.at[1],
             device_id=(sib,), device_id_type=MESH)
-        part_copy.start()
-        sig_ref[1] = sig_ref[1] + s_stage(1, core)
+        for what, first_arg, second_arg, third_arg in ORDER[lead:]:
+            if what == "own":
+                send_own(first_arg, second_arg)
+            elif what == "ev":
+                arrival(first_arg, second_arg, third_arg)
+            elif what == "left":
+                left_part(first_arg)
+            elif what == "mid":
+                mid_part(first_arg)
+            else:
+                right_part(first_arg)
+                if first_arg == 2:
+                    part_copy.start()
         part_copy.wait()
         for cc in range(2):
             pair_copy(cc).wait_send()
@@ -355,11 +375,9 @@
             sig = sig_ref[1, rows, :] + part_ref[rows, :]
             vec = v_ref[cur, rows, :]
             w_ref[rows, :] = sig
-            return accs[0] + fold(sig * vec), accs[1] + fold(vec * vec)
-
-        acc_p, acc_v = lax.fori_loop(0, 16, dots, (zero_acc, zero_acc))
-        dot_val = jnp.sum(acc_p)
-        sq_v = jnp.sum(acc_v)
+            return accs + fold(sig * vec)
+
+        dot_val = jnp.sum(lax.fori_loop(0, 16, dots, zero_acc))
         proj_vec = jnp.full((1, 128), dot_val, F32) / jnp.full((1, 128), jnp.where(sq_v > 0.0, sq_v, 1.0), F32)
         new_proj = jnp.where(sq_v > 0.0, jnp.max(proj_vec), 0.0)
         beta_use = jnp.where(j > 0, beta, 0.0)
@@ -423,8 +441,8 @@
                 pltpu.VMEM((3, 256, 512), F32),
                 pltpu.VMEM((256, 512), F32),
                 pltpu.VMEM((32, 1, 128), F32),
-                pltpu.SemaphoreType.DMA((16, 4)),
-                pltpu.SemaphoreType.DMA((4,)),
+                pltpu.SemaphoreType.DMA((16, 8)),
+                pltpu.SemaphoreType.DMA((8,)),
                 pltpu.SemaphoreType.DMA((2,)),
                 pltpu.SemaphoreType.DMA((2,)),
                 pltpu.SemaphoreType.DMA((2,)),

time: 391 us -> 314 us (0.80)
  Pallas kernels: 379 us -> 302 us
    pallas_call x1, Pallas kernels: 379 us -> 302 us  [local_run(): pl.pallas_call(functools.partial(lanczos_kernel, vec_count), out_shape=(j...]
where the time goes in v2:
time: 314 us
  Pallas kernels  302 us (96%)
  local copies, waits for them, and re-layouts  11.1 us (4%)
    pallas_call x1, Pallas kernels, local_run(): pl.pallas_call(functools.partial(lanczos_kernel, vec_count), out_shape=(j...  302 us

profile of v2, /device:TPU:0, one launch (start us, length us, event | category | flops | bytes accessed | tf_op | source)
XLA Modules:
  0.0 314.2 jit_solution(1668441456389117730)
XLA Ops:
  0.6 1.6 copy.8.op_ref
  2.3 2.1 copy.10
  4.4 302.5 %shard_map.67 = (f32[7,256,512]{2,1,0:T(8,128)}, f32[6]{0:T(128)}, f32[6]{0:T(128)}) custom-call(f32[256,512]{1,0:T(8,128)} %bitcast.11, bf16[32,16,512]{2,1,0:T(8,128)(2,1)} %left_ref.1, bf16[32,16,16]{2,1,0:T(8,128)(2,1)} %copy.8.op_ref, bf16[32,512,512]{2,1,0:T(8,128)(2,1)} %right_ref.1), custom_call_target="tpu_custom_call" | custom-call | tf_op jit(solution)/shard_map/pallas_call | solution.py:413
  306.9 0.0 copy-start.1
  306.9 0.0 copy-start
  306.9 6.3 %copy.11 = f32[7,16,4,4,512]{4,3,2,1,0:T(4,128)} copy(f32[7,16,4,4,512]{4,1,3,2,0:T(8,128)} %bitcast.10) | data formatting | bytes 7340032 | tf_op jit(solution)/shard_map/reshape | solution.py:456
  313.2 0.0 copy-done.1
  313.2 0.5 copy.14
  313.7 0.0 copy-done
  313.7 0.5 copy.15
Async XLA Ops:
  306.9 6.3 %copy-start.1 = (f32[6]{0:T(128)S(1)}, f32[6]{0:T(128)}, u32[]{:S(2)}) copy-start(f32[6]{0:T(128)} %get-tuple-element.13) | copy-start | bytes 76
  306.9 6.8 %copy-start = (f32[6]{0:T(128)S(1)}, f32[6]{0:T(128)}, u32[]{:S(2)}) copy-start(f32[6]{0:T(128)} %get-tuple-element.14) | copy-start | bytes 76

commit v3 on v2

v3 whole, which is shorter than its diff:
```python
import functools

import jax
import jax.numpy as jnp
from jax import lax
from jax.experimental import pallas as pl
from jax.experimental.pallas import tpu as pltpu
from jax.sharding import PartitionSpec as P

NUM_STEPS = 6
MESH = pl.DeviceIdType.MESH
F32 = jnp.float32
BF16 = jnp.bfloat16

ROUTES = ("xzy", "yzx", "zyx", "zxy", "zxy", "zyx", "yxz", "zxy")
ORDER = (
    "o1y", "o1x", "o5y", "o3z", "o5x", "o6y", "o7z", "o0x", "o3y", "o2x", "o2z", "o4z", "o4y", "o3x", "o1z", "o0y",
    "o0z", "o7y", "o6x", "e3n1", "e1y0", "o2y", "e2n1", "e0x0", "e0n1", "e1n1", "e3n2", "e2n2", "e1x0", "e4y0",
    "e6y0", "e7n1", "e2y0", "e0n2", "e1y1", "e2x0", "e2y1", "e3y1", "e0x1", "e3x1", "e3n3", "e6x0", "e3x0", "e3x2",
    "e2y2", "e1n2", "e7n2", "e0x2", "e2d0", "e0y1", "o7x", "o5z", "e3x3", "e2n3", "e1x1", "e4n1", "e1n3", "e7n3",
    "e3d3", "e0y0", "e1d0", "e1y2", "e0d1", "e3y2", "e6d0", "o6z", "e2d1", "e0x3", "e2y3", "e2x3", "e4n2", "e0n3",
    "e1d1", "e2d2", "e7y0", "e7y3", "e2x2", "e5n1", "o4x", "e0d3", "e7x3", "e0d0", "e3y0", "e1y3", "e4n3", "e5n2",
    "e2x1", "e2d3", "l2", "e6y1", "e6n1", "e5n3", "e5x0", "e6x1", "e1d2", "e3d1", "e0d2", "e3d0", "e3d2", "e3y3",
    "e1x2", "e7x0", "e6d1", "l3", "e0y3", "e0y2", "e1x3", "e6y2", "e7x2", "e5y0", "e7x1", "l0", "e1d3", "e6n2", "l1",
    "e5y1", "e6x2", "e4y2", "e4x2", "e5y2", "e4x3", "m0", "e4x0", "e4x1", "m1", "m2", "e4y3", "m3", "e6d2", "e5y3",
    "e7y1", "r0", "r1", "e7d0", "e6x3", "e5x1", "e6d3", "e7d2", "e6y3", "e7d1", "e6n3", "e5x3", "e5d2", "e7d3",
    "e7y2", "l6", "e4d3", "l7", "e5d3", "e5x2", "e4d2", "e4d0", "e5d1", "e5d0", "l5", "e4d1", "e4y1", "l4", "m4",
    "m5", "m6", "m7", "r2", "r3",
)


CLASSES = "nxyd"


def onward(route, cls, dist):
    if route[0] == "z":
        first, second = route[1], route[2]
    elif route[2] == "z":
        first, second = route[0], route[1]
    else:
        first, second = route[0], route[2]
    bit = {"x": 1, "y": 2}
    off_first, off_second = bool(cls & bit[first]), bool(cls & bit[second])
    if route[0] == "z":
        if cls == 0:
            return ["z", first, second]
        return [second] if off_first and not off_second else []
    if route[2] == "z":
        ways = []
        if dist == 0 and cls == 0:
            ways = [first, second]
        elif dist == 0 and off_first and not off_second:
            ways = [second]
        return ways + ["z"]
    if off_second:
        return []
    return ([first] if dist == 0 and not off_first else []) + [second, "z"]


def sends_on(way, cc, pz):
    count = 0
    for piece in range(4 * cc, 4 * cc + 4):
        for cls in range(4):
            for src_z in range(4):
                ways = onward(ROUTES[piece], cls, abs(pz - src_z))
                if way in ("x", "y"):
                    count += way in ways
                elif way == "up":
                    count += "z" in ways and src_z <= pz < 3
                else:
                    count += "z" in ways and src_z >= pz > 0
    return count


def lanczos_kernel(
    vec_count,
    psi_ref, left_ref, op_hbm, right_ref,
    out_ref, alpha_ref, beta_ref,
    u_ref, stage_ref, env_l, env_r, kron_ref, x_ref, y_ref, sig_ref, part_ref, v_ref, w_ref, stat_ref, op_ref, turn_ref, flat_ref,
    recv_sem, send_sem, pair_send, pair_recv, part_sem, stat_sem, load_sem, out_sem, psi_sem,
):
    idx = lax.axis_index("rows")
    core = lax.rem(idx, 2)
    pos_x = lax.rem(idx // 2, 2)
    pos_y = lax.rem(idx // 4, 2)
    pos_z = idx // 8
    chip = idx // 2
    sib = idx + 1 - 2 * core
    next_x = idx + 2 - 4 * pos_x
    next_y = idx + 4 - 8 * pos_y

    def block(piece, first_row, rows):
        return u_ref.at[piece // 4, pl.ds(2 * (piece % 4), 2), pl.ds(pl.multiple_of(first_row, 16), rows), :]

    WAYS = {"x": 0, "y": 1, "up": 2, "down": 3}

    def copy(piece, src, way, first_row, rows):
        target = {"x": next_x, "y": next_y, "up": idx + 8, "down": idx - 8}[way]
        ref = block(piece, first_row, rows)
        return pltpu.make_async_remote_copy(
            src_ref=ref, dst_ref=ref, send_sem=send_sem.at[WAYS[way] + 4 * (piece // 4)],
            recv_sem=recv_sem.at[src, piece], device_id=(target,), device_id_type=MESH)

    def send(piece, src, way, first_row=None, rows=32):
        if first_row is None:
            first_row = 32 * src
        if way == "up":
            @pl.when(pos_z < 3)
            def _():
                copy(piece, src, way, first_row, rows).start()
        elif way == "down":
            @pl.when(pos_z > 0)
            def _():
                copy(piece, src, way, first_row, rows).start()
        else:
            copy(piece, src, way, first_row, rows).start()

    def send_own(piece, way, first_row=None, rows=32):
        for one in (("up", "down") if way == "z" else (way,)):
            send(piece, chip, one, first_row, rows)

    def arrival(piece, cls, dist):
        col_x = 1 - pos_x if cls & 1 else pos_x
        col_y = 1 - pos_y if cls & 2 else pos_y

        def act(src_z, heading):
            src = (src_z * 2 + col_y) * 2 + col_x
            copy(piece, src, "x", 32 * src, 32).wait_recv()
            for way in onward(ROUTES[piece], cls, dist):
                if way != "z":
                    send(piece, src, way)
                else:
                    for one in heading:
                        send(piece, src, one)

        if dist == 0:
            act(pos_z, ("up", "down"))
            return

        @pl.when(pos_z >= dist)
        def _():
            act(pos_z - dist, ("up",))

        @pl.when(pos_z + dist <= 3)
        def _():
            act(pos_z + dist, ("down",))

    def sends_done():
        def wait(count, way, cc):
            if count:
                ref = env_r.at[0, pl.ds(0, count), pl.ds(0, 32), :]
                pltpu.make_async_copy(ref, ref, send_sem.at[WAYS[way] + 4 * cc]).wait()

        for cc in range(2):
            wait(sends_on("x", cc, 0), "x", cc)
            wait(sends_on("y", cc, 0), "y", cc)
        for pz in range(4):
            @pl.when(pos_z == pz)
            def _():
                for cc in range(2):
                    wait(sends_on("up", cc, pz), "up", cc)
                    wait(sends_on("down", cc, pz), "down", cc)

    my_rows = pl.ds(pl.multiple_of(32 * chip + 16 * core, 16), 16)
    right_loads = [
        pltpu.make_async_copy(
            right_ref.at[:, pl.ds(pl.multiple_of(256 * core + 128 * cc, 128), 128), :], env_r.at[cc], load_sem.at[cc])
        for cc in range(2)]
    left_load = pltpu.make_async_copy(left_ref, env_l.at[:, core], load_sem.at[2])
    left_send = pltpu.make_async_remote_copy(
        src_ref=left_ref, dst_ref=env_l.at[:, core], send_sem=load_sem.at[3], recv_sem=load_sem.at[4],
        device_id=(sib,), device_id_type=MESH)
    left_send.start()
    left_load.start()
    psi_loads = [
        pltpu.make_async_copy(psi_ref.at[:, q // 4, q % 4, :], w_ref.at[pl.ds(16 * q, 16), :], psi_sem) for q in range(16)]
    for load in psi_loads:
        load.start()
    op_load = pltpu.make_async_copy(op_hbm, op_ref, load_sem.at[5])
    op_load.start()
    for load in right_loads:
        load.start()

    def build_kron():
        big_row = lax.broadcasted_iota(jnp.int32, (256, 256), 0)
        big_col = lax.broadcasted_iota(jnp.int32, (256, 256), 1)
        row_hi, row_lo = lax.shift_right_logical(big_row, 4), big_row & 15
        col_hi, col_lo = lax.shift_right_logical(big_col, 4), big_col & 15
        spread = jnp.where(row_lo == col_hi, 1.0, 0.0).astype(BF16)
        flat_ref[...] = jnp.transpose(op_ref[...].reshape(256, 32).astype(F32))

        def some(k8, carry):
            for kk in range(8):
                k = k8 * 8 + kk
                tall = jnp.where(row_hi == col_hi, flat_ref[pl.ds(k, 1), :], 0.0).astype(BF16)
                full = jnp.dot(tall, spread, preferred_element_type=F32)
                kron_ref[k] = jnp.where(row_lo == col_lo, full, 0.0).astype(BF16)
            return carry

        lax.fori_loop(0, 4, some, 0)

    def left_part(piece):
        for sub in range(2):
            rp = 2 * (piece % 4) + sub
            out = jnp.dot(env_l[...].reshape(1024, 512), u_ref[piece // 4, rp], preferred_element_type=F32)
            out = out.astype(BF16).reshape(32, 2, 16, 256)
            for ag in range(2):
                for par in range(2):
                    row = (2 * rp + par) * 16
                    x_ref[:, row:row + 16, ag * 128:(ag + 1) * 128] = out[:, ag, :, par * 128:(par + 1) * 128]

    def mid_part(part):
        for kk in range(8):
            k = 8 * (part % 4) + kk
            out = jnp.dot(kron_ref[k], x_ref[k], preferred_element_type=F32).astype(BF16)
            for ag in range(2):
                y_ref[ag, :, k * 128:(k + 1) * 128] = out[:, ag * 128:(ag + 1) * 128]

    def right_part(part):
        cc, who = part // 2, part % 2
        ag = 1 - core if who == 0 else core
        out = jnp.dot(y_ref[ag], env_r[cc].reshape(4096, 512), preferred_element_type=F32)
        sig_ref[who] = out if cc == 0 else sig_ref[who] + out

    lane = lax.broadcasted_iota(jnp.int32, (1, 128), 1)

    def total(val):
        cols = val.shape[1]
        part = val[:, 0:128]
        for first in range(128, cols, 128):
            part = part + val[:, first:first + 128]
        return jnp.sum(jnp.sum(part, axis=0, keepdims=True), axis=1, keepdims=True)

    def start_stats(dot_val, proj, sq_w, sq_v, cross):
        row = jnp.where(lane == 0, dot_val, 0.0)
        for which, val in ((1, proj), (2, sq_w), (3, sq_v), (4, cross)):
            row = jnp.where(lane == which, val, row)
        stat_ref[idx] = row

        def to_all(off, carry):
            pltpu.make_async_remote_copy(
                src_ref=stat_ref.at[idx], dst_ref=stat_ref.at[idx], send_sem=stat_sem.at[0], recv_sem=stat_sem.at[1],
                device_id=(lax.rem(idx + off, 32),), device_id_type=MESH).start()
            return carry

        lax.fori_loop(1, 32, to_all, 0)

    def finish_stats():
        others = stat_ref.at[pl.ds(0, 31)]
        pltpu.make_async_copy(others, others, stat_sem.at[1]).wait()
        pltpu.make_async_copy(others, others, stat_sem.at[0]).wait()

        def pick(row, which):
            return jnp.sum(jnp.where(lane == which, row, 0.0), axis=1, keepdims=True)

        rows = [stat_ref[d] for d in range(32)]
        whole = rows[0]
        for row in rows[1:]:
            whole = whole + row
        alpha = pick(whole, 0) / vec_count
        extra = jnp.zeros((1, 128), F32)
        for row in rows:
            delta = alpha - pltpu.roll(row, 2, 1)
            extra = extra + delta * (delta * row - 2.0 * pltpu.roll(row, 127, 1))
        beta_sq = jnp.sum(jnp.where(lane == 2, whole, jnp.where(lane == 3, extra, 0.0)), axis=1, keepdims=True)
        return alpha, jnp.sqrt(beta_sq / vec_count)

    def fold(val):
        return val[0:8] + val[8:16]

    def normalise(slot, prev, alpha, beta, proj, keep):
        delta = alpha - proj
        scale = 1.0 / beta
        acc = jnp.zeros((8, 512), F32)
        for q in range(16):
            rows = pl.ds(16 * q, 16)
            vec = (w_ref[rows, :] - delta * v_ref[prev, rows, :]) * scale
            v_ref[slot, rows, :] = vec
            acc = acc + fold(vec * vec)
            keep(q, vec)
        return acc

    def turn(slot):
        for q in range(16):
            turn_ref[:, q // 4, q % 4, :] = v_ref[slot, pl.ds(16 * q, 16), :]

    def out_copy(step):
        return pltpu.make_async_copy(turn_ref, out_ref.at[step], out_sem)

    for load in psi_loads:
        load.wait()
    acc = jnp.zeros((8, 512), F32)
    for q in range(16):
        rows = pl.ds(16 * q, 16)
        acc = acc + fold(w_ref[rows, :] * w_ref[rows, :])
        v_ref[1, rows, :] = jnp.zeros((16, 512), F32)
        v_ref[2, rows, :] = jnp.zeros((16, 512), F32)
    nought = jnp.zeros((1, 1), F32)
    start_stats(nought, nought, total(acc), nought, nought)
    op_load.wait()
    build_kron()

    def step_body(j, proj):
        cur = lax.rem(j, 3)
        prev = lax.rem(j + 2, 3)
        alpha, beta = finish_stats()

        def to_bf16(q, vec):
            low, high = vec[:, 0:256], vec[:, 256:512]
            own = jnp.where(core == 0, low, high).astype(BF16)
            far = jnp.where(core == 0, high, low).astype(BF16)
            lanes = slice(q % 2 * 128, q % 2 * 128 + 128)
            for cc in range(2):
                u_ref[cc, q // 2, my_rows, lanes] = own[:, cc * 128:(cc + 1) * 128]
                stage_ref[cc, q // 2, :, lanes] = far[:, cc * 128:(cc + 1) * 128]

        acc_v = normalise(cur, prev, alpha, beta, proj, to_bf16)

        def pair_copy(cc):
            return pltpu.make_async_remote_copy(
                src_ref=stage_ref.at[cc], dst_ref=u_ref.at[cc, :, my_rows, :],
                send_sem=pair_send.at[cc], recv_sem=pair_recv.at[cc], device_id=(sib,), device_id_type=MESH)

        for cc in range(2):
            pair_copy(cc).start()
        lead = 0
        while ORDER[lead][0] == "o":
            lead += 1
        for word in ORDER[:lead]:
            send_own(int(word[1]), word[2], 32 * chip + 16 * core, 16)
        for cc in range(2):
            pair_copy(cc).wait_recv()
            for word in ORDER[:lead]:
                if int(word[1]) // 4 == cc:
                    send_own(int(word[1]), word[2], 32 * chip + 16 * (1 - core), 16)
        sq_v = total(acc_v)

        @pl.when(j > 0)
        def _():
            alpha_ref[j - 1] = alpha[0, 0]
            beta_ref[j - 1] = beta[0, 0]
            out_copy(j - 1).wait()

        turn(cur)
        out_copy(j).start()

        part_copy = pltpu.make_async_remote_copy(
            src_ref=sig_ref.at[0], dst_ref=part_ref, send_sem=part_sem.at[0], recv_sem=part_sem.at[1],
            device_id=(sib,), device_id_type=MESH)
        loaded = False
        for word in ORDER[lead:]:
            what, piece = word[0], int(word[1])
            if what == "o":
                send_own(piece, word[2])
            elif what == "e":
                arrival(piece, CLASSES.index(word[2]), int(word[3]))
            elif what == "l":
                if not loaded:
                    loaded = True

                    @pl.when(j == 0)
                    def _():
                        left_load.wait()
                        left_send.wait()
                        for load in right_loads:
                            load.wait()
                left_part(piece)
            elif what == "m":
                mid_part(piece)
            else:
                right_part(piece)
                if piece == 2:
                    part_copy.start()
        part_copy.wait()
        for cc in range(2):
            pair_copy(cc).wait_send()
        sends_done()

        acc_p = jnp.zeros((8, 512), F32)
        for q in range(16):
            rows = pl.ds(16 * q, 16)
            sig = sig_ref[1, rows, :] + part_ref[rows, :]
            w_ref[rows, :] = sig
            acc_p = acc_p + fold(sig * v_ref[cur, rows, :])
        dot_val = total(acc_p)
        new_proj = jnp.where(sq_v > 0.0, dot_val / jnp.where(sq_v > 0.0, sq_v, 1.0), 0.0)
        beta_use = jnp.where(j > 0, beta, 0.0)
        acc_w = jnp.zeros((8, 512), F32)
        acc_c = jnp.zeros((8, 512), F32)
        for q in range(16):
            rows = pl.ds(16 * q, 16)
            vec = v_ref[cur, rows, :]
            res = w_ref[rows, :] - beta_use * v_ref[prev, rows, :] - new_proj * vec
            w_ref[rows, :] = res
            acc_w = acc_w + fold(res * res)
            acc_c = acc_c + fold(res * vec)
        start_stats(dot_val, new_proj, total(acc_w), sq_v, total(acc_c))
        return new_proj

    proj = lax.fori_loop(0, NUM_STEPS, step_body, nought)
    alpha, beta = finish_stats()
    last = NUM_STEPS % 3
    normalise(last, (NUM_STEPS - 1) % 3, alpha, beta, proj, lambda q, vec: None)
    out_copy(NUM_STEPS - 1).wait()
    turn(last)
    out_copy(NUM_STEPS).start()
    alpha_ref[NUM_STEPS - 1] = alpha[0, 0]
    beta_ref[NUM_STEPS - 1] = beta[0, 0]
    out_copy(NUM_STEPS).wait()


def solution(mesh):
    def local_run(wave_rows, left_rows, op_pair, right_env):
        rows, phys, _, bond = wave_rows.shape
        pair = phys * phys
        vec_count = float(bond * bond * pair)
        op_last = jnp.transpose(op_pair, (1, 2, 0))
        vecs, alpha, beta = pl.pallas_call(
            functools.partial(lanczos_kernel, vec_count),
            out_shape=(
                jax.ShapeDtypeStruct((NUM_STEPS + 1, rows, phys, phys, bond), F32),
                jax.ShapeDtypeStruct((NUM_STEPS,), F32),
                jax.ShapeDtypeStruct((NUM_STEPS,), F32),
            ),
            in_specs=[pl.BlockSpec(memory_space=pl.ANY)] * 4,
            out_specs=(
                pl.BlockSpec(memory_space=pl.ANY),
                pl.BlockSpec(memory_space=pltpu.SMEM),
                pl.BlockSpec(memory_space=pltpu.SMEM),
            ),
            scratch_shapes=[
                pltpu.VMEM((2, 8, 512, 256), BF16),
                pltpu.VMEM((2, 8, 16, 256), BF16),
                pltpu.VMEM((32, 2, 16, 512), BF16),
                pltpu.VMEM((2, 32, 128, 512), BF16),
                pltpu.VMEM((32, 256, 256), BF16),
                pltpu.VMEM((32, 256, 256), BF16),
                pltpu.VMEM((2, 256, 4096), BF16),
                pltpu.VMEM((2, 256, 512), F32),
                pltpu.VMEM((256, 512), F32),
                pltpu.VMEM((3, 256, 512), F32),
                pltpu.VMEM((256, 512), F32),
                pltpu.VMEM((32, 1, 128), F32),
                pltpu.VMEM((16, 16, 32), BF16),
                pltpu.VMEM((16, 4, 4, 512), F32),
                pltpu.VMEM((32, 256), F32),
                pltpu.SemaphoreType.DMA((16, 8)),
                pltpu.SemaphoreType.DMA((8,)),
                pltpu.SemaphoreType.DMA((2,)),
                pltpu.SemaphoreType.DMA((2,)),
                pltpu.SemaphoreType.DMA((2,)),
                pltpu.SemaphoreType.DMA((2,)),
                pltpu.SemaphoreType.DMA((6,)),
                pltpu.SemaphoreType.DMA,
                pltpu.SemaphoreType.DMA,
            ],
            compiler_params=pltpu.CompilerParams(has_side_effects=True, vmem_limit_bytes=60 * 1024 * 1024),
        )(wave_rows, left_rows, op_last, right_env)
        return vecs, alpha, beta

    return jax.shard_map(
        local_run, mesh=mesh,
        in_specs=(P("rows"), P(None, "rows"), P(), P()),
        out_specs=(P(None, "rows"), P(), P()), check_vma=False)
```

time: 314 us -> 293 us (0.933)
  Pallas kernels: 302 us -> 286 us
  local copies, waits for them, and re-layouts: 11.1 us -> 6.22 us
    pallas_call x1, Pallas kernels: 302 us -> 286 us  [local_run(): pl.pallas_call(functools.partial(lanczos_kernel, vec_count), out_shape=(j...]
    reshape x2 -> x0, local copies, waits for them, and re-layouts: 8.39 us -> none  [the longest x1 6.25 us: local_run(): return (vecs.reshape(NUM_STEPS + 1, rows, phys, phys, bond), alpha, beta)]
    unnamed x7, local copies, waits for them, and re-layouts: 2.68 us -> 6.22 us
where the time goes in v3:
time: 293 us
  Pallas kernels  286 us (98%)
  local copies, waits for them, and re-layouts  6.22 us (2%)
    pallas_call x1, Pallas kernels, local_run(): pl.pallas_call(functools.partial(lanczos_kernel, vec_count), out_shape=(j...  286 us
    unnamed x7, local copies, waits for them, and re-layouts  6.22 us

profile of v3, /device:TPU:0, one launch (start us, length us, event | category | flops | bytes accessed | tf_op | source)
XLA Modules:
  0.0 292.8 jit_solution(4999651471844192530)
XLA Ops:
  0.6 286.0 %shard_map.67 = (f32[7,16,4,4,512]{4,3,2,1,0:T(4,128)}, f32[6]{0:T(128)}, f32[6]{0:T(128)}) custom-call(f32[16,4,4,512]{3,2,1,0:T(4,128)} %psi_ref.1, bf16[32,16,512]{2,1,0:T(8,128)(2,1)} %left_ref.1, bf16[16,16,32]{2,1,0:T(8,128)(2,1)} %bitcast.1, bf16[32,512,512]{2,1,0:T(8,128)(2,1)} %right_ref.1), custom_call_target="tpu_custom_call" | custom-call | tf_op jit(solution)/shard_map/pallas_call | solution.py:418
  286.6 0.0 copy-start.1
  286.6 0.0 copy-start
  286.6 5.2 %copy.10 = f32[7,16,4,4,512]{4,3,2,1,0:T(4,128)} copy(f32[7,16,4,4,512]{4,3,2,1,0:T(4,128)} %get-tuple-element.6) | data formatting | bytes 7340032
  291.8 0.0 copy-done.1
  291.8 0.5 copy.11
  292.3 0.0 copy-done
  292.3 0.5 copy.12
Async XLA Ops:
  286.6 5.2 %copy-start.1 = (f32[6]{0:T(128)S(1)}, f32[6]{0:T(128)}, u32[]{:S(2)}) copy-start(f32[6]{0:T(128)} %get-tuple-element.7) | copy-start | bytes 76
  286.6 5.7 %copy-start = (f32[6]{0:T(128)S(1)}, f32[6]{0:T(128)}, u32[]{:S(2)}) copy-start(f32[6]{0:T(128)} %get-tuple-element.8) | copy-start | bytes 76

commit v4 on v3

--- a/solution.py
+++ b/solution.py
@@ -12,20 +12,20 @@
 F32 = jnp.float32
 BF16 = jnp.bfloat16
 
-ROUTES = ("xzy", "yzx", "zyx", "zxy", "zxy", "zyx", "yxz", "zxy")
+ROUTES = ("zyx", "xzy", "zxy", "zyx", "zyx", "xzy", "zyx", "yxz")
 ORDER = (
-    "o1y", "o1x", "o5y", "o3z", "o5x", "o6y", "o7z", "o0x", "o3y", "o2x", "o2z", "o4z", "o4y", "o3x", "o1z", "o0y",
-    "o0z", "o7y", "o6x", "e3n1", "e1y0", "o2y", "e2n1", "e0x0", "e0n1", "e1n1", "e3n2", "e2n2", "e1x0", "e4y0",
-    "e6y0", "e7n1", "e2y0", "e0n2", "e1y1", "e2x0", "e2y1", "e3y1", "e0x1", "e3x1", "e3n3", "e6x0", "e3x0", "e3x2",
-    "e2y2", "e1n2", "e7n2", "e0x2", "e2d0", "e0y1", "o7x", "o5z", "e3x3", "e2n3", "e1x1", "e4n1", "e1n3", "e7n3",
-    "e3d3", "e0y0", "e1d0", "e1y2", "e0d1", "e3y2", "e6d0", "o6z", "e2d1", "e0x3", "e2y3", "e2x3", "e4n2", "e0n3",
-    "e1d1", "e2d2", "e7y0", "e7y3", "e2x2", "e5n1", "o4x", "e0d3", "e7x3", "e0d0", "e3y0", "e1y3", "e4n3", "e5n2",
-    "e2x1", "e2d3", "l2", "e6y1", "e6n1", "e5n3", "e5x0", "e6x1", "e1d2", "e3d1", "e0d2", "e3d0", "e3d2", "e3y3",
-    "e1x2", "e7x0", "e6d1", "l3", "e0y3", "e0y2", "e1x3", "e6y2", "e7x2", "e5y0", "e7x1", "l0", "e1d3", "e6n2", "l1",
-    "e5y1", "e6x2", "e4y2", "e4x2", "e5y2", "e4x3", "m0", "e4x0", "e4x1", "m1", "m2", "e4y3", "m3", "e6d2", "e5y3",
-    "e7y1", "r0", "r1", "e7d0", "e6x3", "e5x1", "e6d3", "e7d2", "e6y3", "e7d1", "e6n3", "e5x3", "e5d2", "e7d3",
-    "e7y2", "l6", "e4d3", "l7", "e5d3", "e5x2", "e4d2", "e4d0", "e5d1", "e5d0", "l5", "e4d1", "e4y1", "l4", "m4",
-    "m5", "m6", "m7", "r2", "r3",
+    "o2z", "o6x", "o2x", "o3y", "o4x", "o5x", "o4z", "o3z", "o2y", "o0z", "o6y", "o0y", "o1x", "o0x", "o1z", "o4y",
+    "o1y", "o7x", "o3x", "o5z", "o7y", "o6z", "e2n1", "e3n1", "e2x0", "e0n1", "e6x0", "e1x0", "e7y0", "e0x0", "e2n2",
+    "e3n2", "e0n2", "o7z", "e1x1", "e3y1", "e2x1", "e2d0", "e7x0", "e2y0", "e4n1", "e1n1", "e4y0", "e2x2", "e3n3",
+    "e7d0", "e0n3", "e2n3", "e1x2", "e3y2", "e3y0", "e0y0", "e0y1", "e0x2", "e2x3", "e3x3", "e3y3", "e4n2", "e1x3",
+    "e1d0", "e1n2", "e3x0", "e4n3", "e5x0", "e0y2", "e1n3", "e0y3", "e2y2", "e4x0", "e6n1", "e3x1", "e2y1", "e3d3",
+    "e7y1", "e0x3", "e3d2", "e2d3", "e7n1", "e6n2", "e5n1", "e1y1", "e2d2", "e1d1", "e4y3", "e3d0", "e7d1", "e6n3",
+    "e2d1", "e3d1", "e0x1", "e1d3", "e0d1", "e5x1", "e7x1", "e2y3", "e4x3", "l2", "e1y0", "e4y2", "e4x2", "e0d3",
+    "e3x2", "e4y1", "e0d0", "l3", "e0d2", "e5n2", "l0", "e7d2", "e1y2", "e1d2", "e6y0", "e1y3", "l1", "e4x1", "e5x2",
+    "e7y2", "m0", "m1", "e6y2", "e6y1", "e6x2", "e7n2", "m2", "m3", "e7x2", "e5n3", "o5y", "e4d2", "e6y3", "e4d3",
+    "r0", "e5x3", "e4d0", "e7d3", "r1", "e6x3", "e5d1", "e4d1", "l4", "e7n3", "e5y3", "e6d2", "e7x3", "e5d0", "e6d0",
+    "e6x1", "e7y3", "l7", "e6d3", "e6d1", "l6", "e5d3", "e5y0", "e5y1", "e5y2", "e5d2", "l5", "m4", "m5", "m6", "m7",
+    "r2", "r3",
 )
 
 
@@ -222,6 +222,11 @@
         out = jnp.dot(y_ref[ag], env_r[cc].reshape(4096, 512), preferred_element_type=F32)
         sig_ref[who] = out if cc == 0 else sig_ref[who] + out
 
+    def right_half(half):
+        lanes = slice(256 * half, 256 * half + 256)
+        rhs = env_r[1, :, :, lanes].reshape(4096, 256)
+        sig_ref[0, :, lanes] = sig_ref[0, :, lanes] + jnp.dot(y_ref[1 - core], rhs, preferred_element_type=F32)
+
     lane = lax.broadcasted_iota(jnp.int32, (1, 128), 1)
 
     def total(val):
@@ -237,13 +242,16 @@
             row = jnp.where(lane == which, val, row)
         stat_ref[idx] = row
 
-        def to_all(off, carry):
+        flips = [(1 - pos_x if m & 2 else pos_x) * 2 + (1 - core if m & 1 else core) for m in range(4)]
+        flips += [flip + 4 * (1 - pos_y) for flip in flips[:4]]
+        flips = [flip + 4 * pos_y for flip in flips[:4]] + flips[4:]
+        z_low, z_high = lax.rem(pos_z, 2), pos_z // 2
+        for m in range(31, 0, -1):
+            high = 1 - z_high if m & 16 else z_high
+            low = 1 - z_low if m & 8 else z_low
             pltpu.make_async_remote_copy(
                 src_ref=stat_ref.at[idx], dst_ref=stat_ref.at[idx], send_sem=stat_sem.at[0], recv_sem=stat_sem.at[1],
-                device_id=(lax.rem(idx + off, 32),), device_id_type=MESH).start()
-            return carry
-
-        lax.fori_loop(1, 32, to_all, 0)
+                device_id=(16 * high + 8 * low + flips[m % 8],), device_id_type=MESH).start()
 
     def finish_stats():
         others = stat_ref.at[pl.ds(0, 31)]
@@ -328,25 +336,28 @@
             lead += 1
         for word in ORDER[:lead]:
             send_own(int(word[1]), word[2], 32 * chip + 16 * core, 16)
+        sq_v = total(acc_v)
+
+        @pl.when(j > 0)
+        def _():
+            alpha_ref[j - 1] = alpha[0, 0]
+            beta_ref[j - 1] = beta[0, 0]
+            out_copy(j - 1).wait()
+
+        turn(cur)
+        out_copy(j).start()
         for cc in range(2):
             pair_copy(cc).wait_recv()
             for word in ORDER[:lead]:
                 if int(word[1]) // 4 == cc:
                     send_own(int(word[1]), word[2], 32 * chip + 16 * (1 - core), 16)
-        sq_v = total(acc_v)
-
-        @pl.when(j > 0)
-        def _():
-            alpha_ref[j - 1] = alpha[0, 0]
-            beta_ref[j - 1] = beta[0, 0]
-            out_copy(j - 1).wait()
-
-        turn(cur)
-        out_copy(j).start()
-
-        part_copy = pltpu.make_async_remote_copy(
-            src_ref=sig_ref.at[0], dst_ref=part_ref, send_sem=part_sem.at[0], recv_sem=part_sem.at[1],
-            device_id=(sib,), device_id_type=MESH)
+
+        def part_copy(half):
+            lanes = slice(256 * half, 256 * half + 256)
+            return pltpu.make_async_remote_copy(
+                src_ref=sig_ref.at[0, :, lanes], dst_ref=part_ref.at[:, lanes],
+                send_sem=part_sem.at[half], recv_sem=part_sem.at[2 + half], device_id=(sib,), device_id_type=MESH)
+
         loaded = False
         for word in ORDER[lead:]:
             what, piece = word[0], int(word[1])
@@ -370,12 +381,13 @@
             else:
                 right_part(piece)
                 if piece == 2:
-                    part_copy.start()
-        part_copy.wait()
+                    for half in range(2):
+                        part_copy(half).start()
         for cc in range(2):
             pair_copy(cc).wait_send()
         sends_done()
-
+        for half in range(2):
+            part_copy(half).wait()
         acc_p = jnp.zeros((8, 512), F32)
         for q in range(16):
             rows = pl.ds(16 * q, 16)
@@ -448,13 +460,13 @@
                 pltpu.SemaphoreType.DMA((8,)),
                 pltpu.SemaphoreType.DMA((2,)),
                 pltpu.SemaphoreType.DMA((2,)),
-                pltpu.SemaphoreType.DMA((2,)),
+                pltpu.SemaphoreType.DMA((4,)),
                 pltpu.SemaphoreType.DMA((2,)),
                 pltpu.SemaphoreType.DMA((6,)),
                 pltpu.SemaphoreType.DMA,
                 pltpu.SemaphoreType.DMA,
             ],
-            compiler_params=pltpu.CompilerParams(has_side_effects=True, vmem_limit_bytes=60 * 1024 * 1024),
+            compiler_params=pltpu.CompilerParams(has_side_effects=True, vmem_limit_bytes=40 * 1024 * 1024),
         )(wave_rows, left_rows, op_last, right_env)
         return vecs, alpha, beta
 

time: 293 us -> 278 us (0.949)
  Pallas kernels: 286 us -> 272 us
    pallas_call x1, Pallas kernels: 286 us -> 272 us  [local_run(): pl.pallas_call(functools.partial(lanczos_kernel, vec_count), out_shape=(j...]
    unnamed x7 -> x9, local copies, waits for them, and re-layouts: 6.22 us -> 5.78 us
where the time goes in v4:
time: 278 us
  Pallas kernels  272 us (98%)
  local copies, waits for them, and re-layouts  5.78 us (2%)
    pallas_call x1, Pallas kernels, local_run(): pl.pallas_call(functools.partial(lanczos_kernel, vec_count), out_shape=(j...  272 us
    unnamed x9, local copies, waits for them, and re-layouts  5.78 us

profile of v4, /device:TPU:0, one launch (start us, length us, event | category | flops | bytes accessed | tf_op | source)
XLA Modules:
  0.0 278.0 jit_solution(1860440022730943024)
XLA Ops:
  0.6 0.0 copy-start
  0.6 1.0 copy-done
  1.7 0.0 copy-start.1
  1.7 1.0 copy-done.1
  2.7 0.0 copy-start.2
  2.7 0.8 copy-done.2
  3.6 271.6 %shard_map.67 = (f32[7,16,4,4,512]{4,3,2,1,0:T(4,128)S(1)}, f32[6]{0:T(128)S(1)}, f32[6]{0:T(128)S(1)}) custom-call(f32[16,4,4,512]{3,2,1,0:T(4,128)S(1)} %copy-done, bf16[32,16,512]{2,1,0:T(8,128)(2,1)S(1)} %copy-done.1, bf16[16,16,32]{2,1,0:T(8,128)(2,1)S(1)} %bitcast.1, bf16[32,512,512]{2,1,0:T(8,128)(2,1)} %right_ref.1), custom_call_target="tpu_custom_call" | custom-call | tf_op jit(solution)/shard_map/pallas_call | solution.py:430
  275.2 1.8 copy.10
  277.0 0.5 copy.11
  277.5 0.5 copy.12
Async XLA Ops:
  0.6 1.0 copy-start
  1.7 1.0 copy-start.1
  2.7 0.8 copy-start.2

commit v5 on v4

--- a/solution.py
+++ b/solution.py
@@ -12,20 +12,20 @@
 F32 = jnp.float32
 BF16 = jnp.bfloat16
 
-ROUTES = ("zyx", "xzy", "zxy", "zyx", "zyx", "xzy", "zyx", "yxz")
+ROUTES = ("zyx", "zyx", "xzy", "zyx", "xzy", "zxy", "zyx", "yxz")
 ORDER = (
-    "o2z", "o6x", "o2x", "o3y", "o4x", "o5x", "o4z", "o3z", "o2y", "o0z", "o6y", "o0y", "o1x", "o0x", "o1z", "o4y",
-    "o1y", "o7x", "o3x", "o5z", "o7y", "o6z", "e2n1", "e3n1", "e2x0", "e0n1", "e6x0", "e1x0", "e7y0", "e0x0", "e2n2",
-    "e3n2", "e0n2", "o7z", "e1x1", "e3y1", "e2x1", "e2d0", "e7x0", "e2y0", "e4n1", "e1n1", "e4y0", "e2x2", "e3n3",
-    "e7d0", "e0n3", "e2n3", "e1x2", "e3y2", "e3y0", "e0y0", "e0y1", "e0x2", "e2x3", "e3x3", "e3y3", "e4n2", "e1x3",
-    "e1d0", "e1n2", "e3x0", "e4n3", "e5x0", "e0y2", "e1n3", "e0y3", "e2y2", "e4x0", "e6n1", "e3x1", "e2y1", "e3d3",
-    "e7y1", "e0x3", "e3d2", "e2d3", "e7n1", "e6n2", "e5n1", "e1y1", "e2d2", "e1d1", "e4y3", "e3d0", "e7d1", "e6n3",
-    "e2d1", "e3d1", "e0x1", "e1d3", "e0d1", "e5x1", "e7x1", "e2y3", "e4x3", "l2", "e1y0", "e4y2", "e4x2", "e0d3",
-    "e3x2", "e4y1", "e0d0", "l3", "e0d2", "e5n2", "l0", "e7d2", "e1y2", "e1d2", "e6y0", "e1y3", "l1", "e4x1", "e5x2",
-    "e7y2", "m0", "m1", "e6y2", "e6y1", "e6x2", "e7n2", "m2", "m3", "e7x2", "e5n3", "o5y", "e4d2", "e6y3", "e4d3",
-    "r0", "e5x3", "e4d0", "e7d3", "r1", "e6x3", "e5d1", "e4d1", "l4", "e7n3", "e5y3", "e6d2", "e7x3", "e5d0", "e6d0",
-    "e6x1", "e7y3", "l7", "e6d3", "e6d1", "l6", "e5d3", "e5y0", "e5y1", "e5y2", "e5d2", "l5", "m4", "m5", "m6", "m7",
-    "r2", "r3",
+    "o1z", "o7x", "o0y", "o7y", "o5x", "o0z", "o5y", "o3x", "o6z", "o1x", "o1y", "o3y", "o2x", "o4y", "o3z", "o2z",
+    "o0x", "o5z", "o4x", "e1n1", "e0n1", "e7y0", "e3y0", "e3n1", "e4x0", "e1n2", "e0n2", "e0y0", "e2n1", "e3n2",
+    "e1y0", "e6n1", "e2x0", "o6y", "e1n3", "e3n3", "o4z", "e0n3", "e1y1", "e1x0", "e5x0", "e1y2", "e2n2", "e3d0",
+    "e1y3", "e7x0", "e2n3", "e2x1", "e7d0", "e3y2", "e0x3", "o7z", "e1x2", "e1x1", "e0y3", "e0y1", "e0y2", "o2y",
+    "e1x3", "e3y3", "e0x1", "e2x2", "e0x0", "e3x0", "e1d0", "e3y1", "e6n2", "e4d0", "e5n1", "e2x3", "e4x1", "e1d3",
+    "e2d0", "e6n3", "e5n2", "e4n1", "e6x1", "e3x1", "e7x1", "e3x3", "e1d1", "e4x2", "e1d2", "e0d0", "e3d3", "e5n3",
+    "e2y3", "o6x", "e6y0", "e2y0", "e3x2", "l1", "e7y1", "e2y1", "e4n2", "e7n1", "e2d3", "e0d1", "e2y2", "e7d1",
+    "e2d2", "e0d3", "e2d1", "e0x2", "e6y1", "e0d2", "l2", "e3d2", "e3d1", "l3", "e7x2", "l0", "e6y3", "m0", "e4x3",
+    "e7y2", "e5y1", "e5y0", "m1", "m2", "e4n3", "e5x3", "e6y2", "e7n2", "e5x1", "m3", "e5x2", "r0", "e4d1", "e7d2",
+    "e6x2", "e5y2", "e4y1", "r1", "e6x3", "e4y3", "e4d3", "e6d3", "e4y2", "e7y3", "e4d2", "e4y0", "l4", "e6d2",
+    "e5d0", "e6x0", "e6d0", "e6d1", "l6", "e5y3", "e7n3", "e7d3", "e5d1", "e7x3", "l7", "e5d2", "e5d3", "l5", "m4",
+    "m5", "m6", "m7", "r2", "r3",
 )
 
 

time: 278 us -> 277 us (level)
  no operation moved by 1% of the time
where the time goes in v5:
time: 277 us
  Pallas kernels  271 us (98%)
  local copies, waits for them, and re-layouts  5.78 us (2%)
    pallas_call x1, Pallas kernels, local_run(): pl.pallas_call(functools.partial(lanczos_kernel, vec_count), out_shape=(j...  271 us
    unnamed x9, local copies, waits for them, and re-layouts  5.78 us

profile of v5, /device:TPU:0, one launch (start us, length us, event | category | flops | bytes accessed | tf_op | source)
XLA Modules:
  0.0 277.0 jit_solution(8521346051846752185)
XLA Ops:
  0.6 0.0 copy-start
  0.6 1.0 copy-done
  1.7 0.0 copy-start.1
  1.7 1.0 copy-done.1
  2.7 0.0 copy-start.2
  2.7 0.8 copy-done.2
  3.6 270.6 %shard_map.67 = (f32[7,16,4,4,512]{4,3,2,1,0:T(4,128)S(1)}, f32[6]{0:T(128)S(1)}, f32[6]{0:T(128)S(1)}) custom-call(f32[16,4,4,512]{3,2,1,0:T(4,128)S(1)} %copy-done, bf16[32,16,512]{2,1,0:T(8,128)(2,1)S(1)} %copy-done.1, bf16[16,16,32]{2,1,0:T(8,128)(2,1)S(1)} %bitcast.1, bf16[32,512,512]{2,1,0:T(8,128)(2,1)} %right_ref.1), custom_call_target="tpu_custom_call" | custom-call | tf_op jit(solution)/shard_map/pallas_call | solution.py:430
  274.2 1.8 copy.10
  276.0 0.5 copy.11
  276.5 0.5 copy.12
Async XLA Ops:
  0.6 1.0 copy-start
  1.7 1.0 copy-start.1
  2.7 0.8 copy-start.2

commit v6 on v4

--- a/solution.py
+++ b/solution.py
@@ -14,18 +14,18 @@
 
 ROUTES = ("zyx", "xzy", "zxy", "zyx", "zyx", "xzy", "zyx", "yxz")
 ORDER = (
-    "o2z", "o6x", "o2x", "o3y", "o4x", "o5x", "o4z", "o3z", "o2y", "o0z", "o6y", "o0y", "o1x", "o0x", "o1z", "o4y",
-    "o1y", "o7x", "o3x", "o5z", "o7y", "o6z", "e2n1", "e3n1", "e2x0", "e0n1", "e6x0", "e1x0", "e7y0", "e0x0", "e2n2",
-    "e3n2", "e0n2", "o7z", "e1x1", "e3y1", "e2x1", "e2d0", "e7x0", "e2y0", "e4n1", "e1n1", "e4y0", "e2x2", "e3n3",
-    "e7d0", "e0n3", "e2n3", "e1x2", "e3y2", "e3y0", "e0y0", "e0y1", "e0x2", "e2x3", "e3x3", "e3y3", "e4n2", "e1x3",
-    "e1d0", "e1n2", "e3x0", "e4n3", "e5x0", "e0y2", "e1n3", "e0y3", "e2y2", "e4x0", "e6n1", "e3x1", "e2y1", "e3d3",
-    "e7y1", "e0x3", "e3d2", "e2d3", "e7n1", "e6n2", "e5n1", "e1y1", "e2d2", "e1d1", "e4y3", "e3d0", "e7d1", "e6n3",
-    "e2d1", "e3d1", "e0x1", "e1d3", "e0d1", "e5x1", "e7x1", "e2y3", "e4x3", "l2", "e1y0", "e4y2", "e4x2", "e0d3",
-    "e3x2", "e4y1", "e0d0", "l3", "e0d2", "e5n2", "l0", "e7d2", "e1y2", "e1d2", "e6y0", "e1y3", "l1", "e4x1", "e5x2",
-    "e7y2", "m0", "m1", "e6y2", "e6y1", "e6x2", "e7n2", "m2", "m3", "e7x2", "e5n3", "o5y", "e4d2", "e6y3", "e4d3",
-    "r0", "e5x3", "e4d0", "e7d3", "r1", "e6x3", "e5d1", "e4d1", "l4", "e7n3", "e5y3", "e6d2", "e7x3", "e5d0", "e6d0",
-    "e6x1", "e7y3", "l7", "e6d3", "e6d1", "l6", "e5d3", "e5y0", "e5y1", "e5y2", "e5d2", "l5", "m4", "m5", "m6", "m7",
-    "r2", "r3",
+    "o3z", "o4y", "o0z", "o2y", "o1x", "o5y", "o1y", "o4z", "o2x", "o6x", "o2z", "o1z", "o7y", "o0y", "o7x", "o6z",
+    "o3y", "o5x", "e3n1", "e0n1", "e2n1", "e1y0", "e1x0", "e2x0", "e7y0", "o6y", "e3n2", "e3y0", "e3x1", "e5y0",
+    "e2n2", "o0x", "e7x0", "e0n2", "e3n3", "e5x0", "e4n1", "e0y0", "o3x", "e2n3", "e1x1", "e0n3", "e0y1", "e1n1",
+    "o5z", "e3y2", "e3y3", "o7z", "e3d0", "e3x2", "e1x2", "e2x3", "e7d0", "e3y1", "e2x2", "e6y0", "e2y1", "e1n2",
+    "e0y3", "e1x3", "e6x0", "e0y2", "e1n3", "e2x1", "e4n2", "e6n1", "e4n3", "e6n3", "e5d0", "e4y1", "e0d0", "e6n2",
+    "e0x2", "e5n1", "e5x1", "e7d1", "e3x3", "e7x1", "e5n2", "e1d0", "e3d1", "e3d3", "e2y0", "e0d3", "e0x0", "e3d2",
+    "e7y1", "e2d2", "e1d2", "e3x0", "l3", "e5x2", "e0x3", "e0d1", "e0x1", "e2d0", "e2y3", "e0d2", "o4x", "l0", "e7n1",
+    "e2d3", "e1d3", "e1y3", "e2y2", "e7d2", "e1d1", "e6d0", "e1y1", "e1y2", "e2d1", "l2", "l1", "e5n3", "e4x3",
+    "e4y3", "m0", "e4y0", "e4y2", "e7x2", "m1", "e6x3", "e6y1", "m2", "m3", "e7y2", "e5x3", "e6y3", "e6y2", "e7n2",
+    "e6x1", "r0", "e4d1", "e4d3", "r1", "e5d1", "e4x2", "e4d2", "e7y3", "e7x3", "e4x1", "e7d3", "e4x0", "e4d0", "l4",
+    "e7n3", "e5y3", "l7", "e5y2", "e6d1", "e5y1", "e6x2", "e5d2", "e5d3", "l5", "e6d2", "e6d3", "l6", "m4", "m5",
+    "m6", "m7", "r2", "r3",
 )
 
 

time: 278 us -> 278 us (level)
  no operation moved by 1% of the time
where the time goes in v6:
time: 278 us
  Pallas kernels  272 us (98%)
  local copies, waits for them, and re-layouts  5.78 us (2%)
    pallas_call x1, Pallas kernels, local_run(): pl.pallas_call(functools.partial(lanczos_kernel, vec_count), out_shape=(j...  272 us
    unnamed x9, local copies, waits for them, and re-layouts  5.78 us

profile of v6, /device:TPU:0, one launch (start us, length us, event | category | flops | bytes accessed | tf_op | source)
XLA Modules:
  0.0 278.2 jit_solution(4205715943463615178)
XLA Ops:
  0.6 0.0 copy-start
  0.6 1.0 copy-done
  1.7 0.0 copy-start.1
  1.7 1.0 copy-done.1
  2.7 0.0 copy-start.2
  2.7 0.8 copy-done.2
  3.6 271.8 %shard_map.67 = (f32[7,16,4,4,512]{4,3,2,1,0:T(4,128)S(1)}, f32[6]{0:T(128)S(1)}, f32[6]{0:T(128)S(1)}) custom-call(f32[16,4,4,512]{3,2,1,0:T(4,128)S(1)} %copy-done, bf16[32,16,512]{2,1,0:T(8,128)(2,1)S(1)} %copy-done.1, bf16[16,16,32]{2,1,0:T(8,128)(2,1)S(1)} %bitcast.1, bf16[32,512,512]{2,1,0:T(8,128)(2,1)} %right_ref.1), custom_call_target="tpu_custom_call" | custom-call | tf_op jit(solution)/shard_map/pallas_call | solution.py:430
  275.4 1.8 copy.10
  277.2 0.5 copy.11
  277.7 0.5 copy.12
Async XLA Ops:
  0.6 1.0 copy-start
  1.7 1.0 copy-start.1
  2.7 0.8 copy-start.2
